TPU v7x, 128 devices: a whole 4x4x4 slice. The times are simulated.
128 devices in a mesh: rep: 1, r: 4 (over x), s: 32 (over y, z, core).
Axes of the slice: x: 4, y: 4, z: 4, core: 2. Of those that a mesh axis runs over, the one named last changes fastest.
Arguments:
- x: bfloat16 [128, 2048, 1280], P(('rep', 'r', 's'))
- dy: bfloat16 [128, 2048, 1280], P(('rep', 'r', 's'))
- w_gate: bfloat16 [2, 1280, 3584], P(None, 's')
- w_up: bfloat16 [2, 1280, 3584], P(None, 's')
- w_down: bfloat16 [2, 3584, 1280], P(None, 's')
- m_w_gate: float32 [2, 1280, 3584], P(None, 's')
- m_w_up: float32 [2, 1280, 3584], P(None, 's')
- m_w_down: float32 [2, 3584, 1280], P(None, 's')
- v_w_gate: float32 [2, 1280, 3584], P(None, 's')
- v_w_up: float32 [2, 1280, 3584], P(None, 's')
- v_w_down: float32 [2, 3584, 1280], P(None, 's')
Outputs:
- output 1: bfloat16 [2, 1280, 3584], P('rep', 's')
- output 2: bfloat16 [2, 1280, 3584], P('rep', 's')
- output 3: bfloat16 [2, 3584, 1280], P('rep', 's')
- output 4: float32 [2, 1280, 3584], P('rep', 's')
- output 5: float32 [2, 1280, 3584], P('rep', 's')
- output 6: float32 [2, 3584, 1280], P('rep', 's')
- output 7: float32 [2, 1280, 3584], P('rep', 's')
- output 8: float32 [2, 1280, 3584], P('rep', 's')
- output 9: float32 [2, 3584, 1280], P('rep', 's')
All inputs are finite; a program needn't handle non-finite values.
Results may differ from a plain program's by a relative error of at most 0.022.
Values are sent between devices in bfloat16 or wider.
A program may use at most 1.5 GiB of HBM per device.

v0:
```python
import jax
import jax.numpy as jnp
from jax import lax
from jax.sharding import PartitionSpec as P

NAMES = ("w_gate", "w_up", "w_down")


def matmul(a, w):
    return jnp.dot(a, w, preferred_element_type=jnp.float32).astype(jnp.bfloat16)


def normed(h):
    wide = h.astype(jnp.float32)
    scale = lax.rsqrt(jnp.mean(wide**2, -1, keepdims=True) + 1e-6)
    return (wide * scale).astype(jnp.bfloat16)


def layer(h, w):
    a = normed(h)
    gate = jnp.dot(a, w["w_gate"], preferred_element_type=jnp.float32)
    up = jnp.dot(a, w["w_up"], preferred_element_type=jnp.float32)
    return h + matmul((jax.nn.silu(gate) * up).astype(jnp.bfloat16), w["w_down"])


def adamw(w, m, v, g):
    m = 0.9 * m + 0.1 * g
    v = 0.95 * v + 0.05 * g * g
    step = m * lax.rsqrt(v + 1e-8) + 0.1 * w
    return (w - 0.02 * step).astype(jnp.bfloat16), m, v


def clipped(gradients, sum_of_squares, count):
    factor = jnp.minimum(1.0, 0.5 * lax.rsqrt(sum_of_squares / count + 1e-30))
    return [g * factor for g in gradients]


def solution(mesh):
    def fetched(weights, number):
        return {name: lax.all_gather(w[number], "s", axis=0, tiled=True) for name, w in zip(NAMES, weights, strict=True)}

    def summed(term):
        return lax.psum(lax.psum_scatter(term, "s", scatter_dimension=0, tiled=True), "r")

    def step(x, dy, *arrays):
        weights, m, v = (arrays[i : i + 3] for i in (0, 3, 6))
        layers = weights[0].shape[0]
        h, kept = x[0], []
        for number in range(layers):
            kept.append(h)
            h = layer(h, fetched(weights, number))
        by_h, mine = dy[0], [None] * layers
        for number in reversed(range(layers)):
            _, back = jax.vjp(lambda w, h: layer(h, w), fetched(weights, number), kept[number])
            by_w, by_h = back(by_h)
            mine[number] = [summed(by_w[name]) for name in NAMES]
        gradients = [jnp.stack([mine[number][i] for number in range(layers)]).astype(jnp.float32) for i in range(3)]
        squares = lax.psum(sum(jnp.sum(g * g) for g in gradients), "s")
        gradients = clipped(gradients, squares, lax.psum(1, "s") * sum(g.size for g in gradients))
        new = [adamw(w.astype(jnp.float32), m, v, g) for w, m, v, g in zip(weights, m, v, gradients, strict=True)]
        return tuple(one[which] for which in range(3) for one in new)

    states, cut = P(("rep", "r", "s"), None, None), P(None, "s", None)
    return jax.shard_map(
        step,
        mesh=mesh,
        in_specs=(states, states) + (cut,) * 9,
        out_specs=(P("rep", "s", None),) * 9,
        check_vma=False,
    )
```

profile of v0, /device:TPU:1, one launch (start us, length us, event | category | flops | bytes accessed | tf_op | source)
XLA Modules:
  0.0 1218.9 jit_solution(14697962760493374240)
XLA Ops:
  34.4 34.5 %all-gather.13.cloned.1.call-done = bf16[1,1280,3584]{2,1,0:T(8,128)(2,1)} async-done(((bf16[1,40,3584]{2,1,0:T(8,128)(2,1)}), bf16[1,1280,3584]{2,1,0:T(8,128)(2,1)}) %all-gather.13.cloned.1.call-update) | async-done | bytes 9175056 | tf_op jit(solution)/shard_map/all_gather | solution.py:40
  68.9 27.0 %fusion.39 = f32[2048,3584]{1,0:T(8,128)} fusion(bf16[1,1280,3584]{2,1,0:T(8,128)(2,1)} %all-gather.13.cloned.1.call-done, bf16[1,2048,1280]{1,2,0:T(8,128)(2,1)} %copy.20, f32[2048]{0:T(1024)S(1)} %add_rsqrt_fusion), kind=kOutput, calls=%fused_computation.58 | convolution fusion | flops 18798346240 | bytes 43786240 | tf_op jit(solution)/shard_map/dot_general | solution.py:21
  95.9 29.8 %all-gather.15.cloned.1.call-done = bf16[1,1280,3584]{2,1,0:T(8,128)(2,1)} async-done(((bf16[1,40,3584]{2,1,0:T(8,128)(2,1)}), bf16[1,1280,3584]{2,1,0:T(8,128)(2,1)}) %all-gather.15.cloned.1.call-update) | async-done | bytes 9175056 | tf_op jit(solution)/shard_map/all_gather | solution.py:40
  125.7 36.4 %multiply_convert_fusion.1 = (bf16[2048,3584]{1,0:T(8,128)(2,1)}, f32[2048,3584]{1,0:T(8,128)}) fusion(f32[2048,3584]{1,0:T(8,128)} %fusion.39, bf16[1,1280,3584]{2,1,0:T(8,128)(2,1)} %all-gather.15.cloned.1.call-done, bf16[1,2048,1280]{1,2,0:T(8,128)(2,1)} %copy.20, f32[2048]{0:T(1024)S(1)} %add_rsqrt_fusion), kind=kOutput, calls=%fused_computation.17 | convolution fusion | flops 18842386432 | bytes 87826432 | tf_op jit(solution)/shard_map/dot_general | solution.py:22
  182.4 27.0 %fusion.23 = (f32[2048]{0:T(1024)S(1)}, bf16[2048,1280]{0,1:T(8,128)(2,1)}) fusion(bf16[2048,3584]{1,0:T(8,128)(2,1)} %get-tuple-element.30, bf16[1,3584,1280]{2,1,0:T(8,128)(2,1)} %all-gather.17.cloned.1.call-done, bf16[1,2048,1280]{1,2,0:T(8,128)(2,1)} %copy.20), kind=kOutput, calls=%fused_computation.42 | convolution fusion | flops 18803587072 | bytes 34349056 | tf_op jit(solution)/shard_map/dot_general | solution.py:10
  210.0 29.1 %all-gather.21.cloned.1.call-done = bf16[1,3584,1280]{2,1,0:T(8,128)(2,1)} async-done(((bf16[1,112,1280]{2,1,0:T(8,128)(2,1)}), bf16[1,3584,1280]{2,1,0:T(8,128)(2,1)}) %all-gather.21.cloned.1.call-update) | async-done | bytes 9175056 | tf_op jit(solution)/shard_map/all_gather | solution.py:40
  265.1 30.6 %all-gather.23.cloned.1.call-done = bf16[1,1280,3584]{2,1,0:T(8,128)(2,1)} async-done(((bf16[1,40,3584]{2,1,0:T(8,128)(2,1)}), bf16[1,1280,3584]{2,1,0:T(8,128)(2,1)}) %all-gather.23.cloned.1.call-update) | async-done | bytes 9175056 | tf_op jit(solution)/shard_map/all_gather | solution.py:40
  295.7 27.1 %fusion.26 = f32[2048,3584]{1,0:T(8,128)} fusion(bf16[1,1280,3584]{2,1,0:T(8,128)(2,1)} %all-gather.23.cloned.1.call-done, bf16[2048,1280]{0,1:T(8,128)(2,1)} %get-tuple-element.33, f32[2048]{0:T(1024)S(1)} %fusion.89), kind=kOutput, calls=%fused_computation.45 | convolution fusion | flops 18798346240 | bytes 43786240 | tf_op jit(solution)/shard_map/jvp()/dot_general | solution.py:22
  322.8 29.5 %all-gather.19.cloned.1.call-done = bf16[1,1280,3584]{2,1,0:T(8,128)(2,1)} async-done(((bf16[1,40,3584]{2,1,0:T(8,128)(2,1)}), bf16[1,1280,3584]{2,1,0:T(8,128)(2,1)}) %all-gather.19.cloned.1.call-update) | async-done | bytes 9175056 | tf_op jit(solution)/shard_map/all_gather | solution.py:40
  352.3 44.2 %fusion.2 = (bf16[2048,3584]{1,0:T(8,128)(2,1)}, f32[2048,3584]{1,0:T(8,128)}) fusion(f32[2048,3584]{1,0:T(8,128)} %fusion.26, bf16[2048,3584]{1,0:T(8,128)(2,1)} %convolution_convert_fusion.4, bf16[1,1280,3584]{2,1,0:T(8,128)(2,1)} %all-gather.19.cloned.1.call-done, bf16[2048,1280]{0,1:T(8,128)(2,1)} %get-tuple-element.33, f32[2048]{0:T(1024)S(1)} %fusion.89), kind=kOutput, calls=%fused_computation.8 | convolution fusion | flops 18886426624 | bytes 102506496 | tf_op jit(solution)/shard_map/jvp()/dot_general | solution.py:21
  396.5 26.3 %fusion.44 = bf16[2048,1280]{0,1:T(8,128)(2,1)} fusion(bf16[2048,3584]{1,0:T(8,128)(2,1)} %get-tuple-element.34, bf16[1,1280,3584]{2,1,0:T(8,128)(2,1)} %all-gather.19.cloned.1.call-done), kind=kOutput, calls=%fused_computation.61 | convolution fusion | flops 18790481920 | bytes 29097984 | tf_op jit(solution)/shard_map/transpose(jvp())/dot_general | solution.py:21
  422.8 31.9 %fusion.25 = (f32[2048]{0:T(1024)S(1)}, bf16[2048,1280]{0,1:T(8,128)(2,1)}) fusion(bf16[2048,1280]{0,1:T(8,128)(2,1)S(1)} %copy-done, bf16[2048,1280]{0,1:T(8,128)(2,1)} %fusion.44, bf16[1,1280,3584]{2,1,0:T(8,128)(2,1)} %all-gather.23.cloned.1.call-done, bf16[2048,3584]{1,0:T(8,128)(2,1)} %convolution_convert_fusion.4, f32[2048,3584]{1,0:T(8,128)} %get-tuple-element.35), kind=kOutput, calls=%fused_computation.44 | convolution fusion | flops 18850248704 | bytes 68952064 | tf_op jit(solution)/shard_map/transpose(jvp())/dot_general | solution.py:22
  492.0 30.9 %convolution_convert_fusion.1 = bf16[3584,1280]{1,0:T(8,128)(2,1)} fusion(f32[2048,3584]{1,0:T(8,128)} %fusion.26, bf16[1,2048,1280]{2,1,0:T(8,128)(2,1)} %param.12, f32[2048,3584]{1,0:T(8,128)} %get-tuple-element.35), kind=kOutput, calls=%fused_computation.30 | convolution fusion | flops 18839109632 | bytes 73138176 | tf_op jit(solution)/shard_map/transpose(jvp())/dot_general | solution.py:10
  522.9 26.2 %convolution_convert_fusion.3 = bf16[2048,3584]{1,0:T(8,128)(2,1)} fusion(bf16[2048,1280]{0,1:T(8,128)(2,1)} %fusion.56, bf16[1,3584,1280]{2,1,0:T(8,128)(2,1)} %all-gather.17.cloned.1.call-done), kind=kOutput, calls=%fused_computation.32 | convolution fusion | flops 18797821952 | bytes 29097984 | tf_op jit(solution)/shard_map/transpose(jvp())/dot_general | solution.py:10
  549.1 30.2 %fusion.17 = bf16[1280,3584]{1,0:T(8,128)(2,1)} fusion(bf16[2048,3584]{1,0:T(8,128)(2,1)} %convolution_convert_fusion.3, f32[2048,3584]{1,0:T(8,128)} %fusion.39, bf16[1,2048,1280]{1,2,0:T(8,128)(2,1)} %copy.20, f32[2048]{0:T(1024)S(1)} %copy-done.10), kind=kOutput, calls=%fused_computation.29 | convolution fusion | flops 18846973952 | bytes 58466304 | tf_op jit(solution)/shard_map/transpose(jvp())/dot_general | solution.py:22
  580.1 30.4 %fusion.16 = bf16[1280,3584]{1,0:T(8,128)(2,1)} fusion(bf16[2048,3584]{1,0:T(8,128)(2,1)} %convolution_convert_fusion.4, bf16[2048,1280]{0,1:T(8,128)(2,1)} %get-tuple-element.33, f32[2048]{0:T(1024)S(1)} %copy-done.6, f32[2048,3584]{1,0:T(8,128)} %get-tuple-element.35), kind=kOutput, calls=%fused_computation.28 | convolution fusion | flops 18846973952 | bytes 58466304 | tf_op jit(solution)/shard_map/transpose(jvp())/dot_general | solution.py:22
  610.5 36.5 %fusion.13 = bf16[1280,3584]{1,0:T(8,128)(2,1)} fusion(f32[2048,3584]{1,0:T(8,128)} %fusion.39, f32[2048,3584]{1,0:T(8,128)} %get-tuple-element.31, bf16[2048,3584]{1,0:T(8,128)(2,1)} %convolution_convert_fusion.3, bf16[1,2048,1280]{1,2,0:T(8,128)(2,1)} %copy.20, f32[2048]{0:T(1024)S(1)} %copy-done.10), kind=kOutput, calls=%fused_computation.26 | convolution fusion | flops 18883674112 | bytes 87826432 | tf_op jit(solution)/shard_map/transpose(jvp())/dot_general | solution.py:21
  647.1 26.4 %convolution_convert_fusion = bf16[1280,3584]{1,0:T(8,128)(2,1)} fusion(bf16[2048,3584]{1,0:T(8,128)(2,1)} %get-tuple-element.34, bf16[2048,1280]{0,1:T(8,128)(2,1)} %get-tuple-element.33, f32[2048]{0:T(1024)S(1)} %copy-done.6), kind=kOutput, calls=%fused_computation.27 | convolution fusion | flops 18798346240 | bytes 29106176 | tf_op jit(solution)/shard_map/transpose(jvp())/dot_general | solution.py:21
  682.6 98.1 %reduce-scatter.11.cloned.1.call-done = bf16[40,3584]{1,0:T(8,128)(2,1)} async-done(((bf16[1280,3584]{1,0:T(8,128)(2,1)}), bf16[40,3584]{1,0:T(8,128)(2,1)}) %reduce-scatter.11.cloned.1.call-update) | async-done | bytes 286736 | tf_op jit(solution)/shard_map/reduce_scatter | solution.py:43
  780.7 98.0 %reduce-scatter.13.cloned.1.call-done = bf16[40,3584]{1,0:T(8,128)(2,1)} async-done(((bf16[1280,3584]{1,0:T(8,128)(2,1)}), bf16[40,3584]{1,0:T(8,128)(2,1)}) %reduce-scatter.13.cloned.1.call-update) | async-done | bytes 286736 | tf_op jit(solution)/shard_map/reduce_scatter | solution.py:43
  878.6 98.1 %reduce-scatter.7.cloned.1.call-done = bf16[40,3584]{1,0:T(8,128)(2,1)} async-done(((bf16[1280,3584]{1,0:T(8,128)(2,1)}), bf16[40,3584]{1,0:T(8,128)(2,1)}) %reduce-scatter.7.cloned.1.call-update) | async-done | bytes 286736 | tf_op jit(solution)/shard_map/reduce_scatter | solution.py:43
  976.8 98.0 %reduce-scatter.9.cloned.1.call-done = bf16[40,3584]{1,0:T(8,128)(2,1)} async-done(((bf16[1280,3584]{1,0:T(8,128)(2,1)}), bf16[40,3584]{1,0:T(8,128)(2,1)}) %reduce-scatter.9.cloned.1.call-update) | async-done | bytes 286736 | tf_op jit(solution)/shard_map/reduce_scatter | solution.py:43
  1074.8 56.3 %all-reduce.3.cloned.1.call-done = (bf16[1,40,3584]{2,1,0:T(8,128)(2,1)}, bf16[1,40,3584]{2,1,0:T(8,128)(2,1)}, bf16[1,40,3584]{2,1,0:T(8,128)(2,1)}, bf16[1,40,...) async-done(((bf16[1,40,3584]{2,1,0:T(8,128)(2,1)}, bf16[1,40,3584]{2,1,0:T(8,128)(2,1)}, bf16[1,40,3584]{2,1,0:T(8,128)(2,1)}, ...) | async-done | bytes 1720336 | tf_op jit(solution)/shard_map/psum | solution.py:43
  1138.9 63.4 %psum.55 = f32[]{:T(128)} all-reduce(f32[]{:T(128)S(6)} %add.111), channel_id=1, replica_groups=mesh['rep'=1,'r'=4,'s'=32] {'s'}, use_global_device_ids=true, to_apply=%region_18.19 | all-reduce | flops 1 | bytes 8 | tf_op jit(solution)/shard_map/psum | solution.py:58
  (68 shorter events, 136.2 us)
Async XLA Ops:
  7.2 61.7 %all-gather.13.cloned.1.call-start = ((), (), s32[]{:S(2)}) async-start(), calls=%async_computation.12 | async-start | bytes 9461760 | tf_op jit(solution)/shard_map/all_gather | solution.py:40
  9.1 116.5 %all-gather.15.cloned.1.call-start = ((), (), s32[]{:S(2)}) async-start(), calls=%async_computation.13 | async-start | bytes 9461760 | tf_op jit(solution)/shard_map/all_gather | solution.py:40
  11.1 171.3 %all-gather.17.cloned.1.call-start = ((), (), s32[]{:S(2)}) async-start(), calls=%async_computation.14 | async-start | bytes 9461760 | tf_op jit(solution)/shard_map/all_gather | solution.py:40
  13.1 226.0 %all-gather.21.cloned.1.call-start = ((), (), s32[]{:S(2)}) async-start(), calls=%async_computation.16 | async-start | bytes 9461760 | tf_op jit(solution)/shard_map/all_gather | solution.py:40
  13.6 282.1 %all-gather.23.cloned.1.call-start = ((), (), s32[]{:S(2)}) async-start(), calls=%async_computation.17 | async-start | bytes 9461760 | tf_op jit(solution)/shard_map/all_gather | solution.py:40
  14.2 338.1 %all-gather.19.cloned.1.call-start = ((), (), s32[]{:S(2)}) async-start(), calls=%async_computation.15 | async-start | bytes 9461760 | tf_op jit(solution)/shard_map/all_gather | solution.py:40
  14.8 658.8 %reduce-scatter.15.cloned.1.call-start = ((), (), s32[]{:S(2)}) async-start(), calls=%async_computation.10 | async-start | bytes 9461760 | tf_op jit(solution)/shard_map/reduce_scatter | solution.py:43
  26.4 99.2 %copy-start.9 = (f32[2048]{0:T(1024)}, f32[2048]{0:T(1024)S(1)}, u32[]{:S(2)}) copy-start(f32[2048]{0:T(1024)S(1)} %add_rsqrt_fusion) | copy-start | bytes 24580
  209.4 0.6 copy-start.7
  210.0 244.7 %copy-start.5 = (f32[2048]{0:T(1024)}, f32[2048]{0:T(1024)S(1)}, u32[]{:S(2)}) copy-start(f32[2048]{0:T(1024)S(1)} %fusion.89) | copy-start | bytes 24580
  396.5 26.3 %copy-start = (bf16[2048,1280]{0,1:T(8,128)(2,1)S(1)}, bf16[2048,1280]{0,1:T(8,128)(2,1)}, u32[]{:S(2)}) copy-start(bf16[2048,1280]{0,1:T(8,128)(2,1)} %get-tuple-element.33) | copy-start | bytes 15728644
  422.8 31.9 %copy-start.8 = (f32[2048]{0:T(1024)S(1)}, f32[2048]{0:T(1024)}, u32[]{:S(2)}) copy-start(f32[2048]{0:T(1024)} %copy-done.7) | copy-start | bytes 24580
  491.9 190.7 %reduce-scatter.17.cloned.1.call-start = ((), (), s32[]{:S(2)}) async-start(), calls=%async_computation.11 | async-start | bytes 9461760 | tf_op jit(solution)/shard_map/reduce_scatter | solution.py:43
  522.9 26.3 %copy-start.10 = (f32[2048]{0:T(1024)S(1)}, f32[2048]{0:T(1024)}, u32[]{:S(2)}) copy-start(f32[2048]{0:T(1024)} %copy-done.9) | copy-start | bytes 24580
  522.9 257.8 %reduce-scatter.11.cloned.1.call-start = ((), (), s32[]{:S(2)}) async-start(), calls=%async_computation.8 | async-start | bytes 9461760 | tf_op jit(solution)/shard_map/reduce_scatter | solution.py:43
  579.4 0.7 copy-start.6
  579.4 299.3 %reduce-scatter.13.cloned.1.call-start = ((), (), s32[]{:S(2)}) async-start(), calls=%async_computation.9 | async-start | bytes 9461760 | tf_op jit(solution)/shard_map/reduce_scatter | solution.py:43
  610.5 366.3 %reduce-scatter.7.cloned.1.call-start = ((), (), s32[]{:S(2)}) async-start(), calls=%async_computation.6 | async-start | bytes 9461760 | tf_op jit(solution)/shard_map/reduce_scatter | solution.py:43
  647.1 427.7 %reduce-scatter.9.cloned.1.call-start = ((), (), s32[]{:S(2)}) async-start(), calls=%async_computation.7 | async-start | bytes 9461760 | tf_op jit(solution)/shard_map/reduce_scatter | solution.py:43
  673.5 529.5 %copy-start.1 = (bf16[2,112,1280]{2,1,0:T(8,128)(2,1)S(1)}, bf16[2,112,1280]{2,1,0:T(8,128)(2,1)}, u32[]{:S(2)}) copy-start(bf16[2,112,1280]{2,1,0:T(8,128)(2,1)} %param.15) | copy-start | bytes 1720324
  673.5 529.5 %copy-start.4 = (f32[2,112,1280]{2,1,0:T(8,128)S(1)}, f32[2,112,1280]{2,1,0:T(8,128)}, u32[]{:S(2)}) copy-start(f32[2,112,1280]{2,1,0:T(8,128)} %param.21) | copy-start | bytes 3440644
  673.5 532.8 %copy-start.2 = (bf16[2,40,3584]{2,1,0:T(8,128)(2,1)S(1)}, bf16[2,40,3584]{2,1,0:T(8,128)(2,1)}, u32[]{:S(2)}) copy-start(bf16[2,40,3584]{2,1,0:T(8,128)(2,1)} %param.13) | copy-start | bytes 1720324
  673.5 532.8 %copy-start.3 = (bf16[2,40,3584]{2,1,0:T(8,128)(2,1)S(1)}, bf16[2,40,3584]{2,1,0:T(8,128)(2,1)}, u32[]{:S(2)}) copy-start(bf16[2,40,3584]{2,1,0:T(8,128)(2,1)} %param.14) | copy-start | bytes 1720324
  673.5 457.6 %all-reduce.3.cloned.1.call-start = ((), (), s32[]{:S(2)}) async-start(), calls=%async_computation.18 | async-start | bytes 3440640 | tf_op jit(solution)/shard_map/psum | solution.py:43
Sparse Core Ops, SparseCore 0:
  10.8 58.0 all-gather.12
  71.7 53.9 all-gather.14
  128.5 53.9 all-gather.16
  185.1 53.9 all-gather.20
  241.7 53.9 all-gather.22
  298.4 53.9 all-gather.18
  492.0 92.3 reduce-scatter.14
  588.2 94.3 reduce-scatter.16
  686.4 94.2 reduce-scatter.10
  784.3 94.2 reduce-scatter.12
  882.4 94.2 reduce-scatter.6
  980.4 94.2 reduce-scatter.8
  1077.5 53.4 all-reduce.2
where the time goes:
time: 1230 us; the launch traced here: 1220 us
  waiting for transfers between devices  633 us (51%)
  matrix products  451 us (37%)
  blocking collectives  63.4 us (5%)
  other arithmetic  30.9 us (3%)
  local copies, waits for them, and re-layouts  22.9 us (2%)
  between operations  16.9 us (1%)
    reduce_scatter x6, waiting for transfers between devices, summed(): lax.psum_scatter(term, 's', scatter_dimension=0, tiled=True)  401 us
    all_gather x6, waiting for transfers between devices, fetched(): lax.all_gather(w[number], 's', axis=0, tiled=True)  174 us
    dot_general x5, matrix products, layer(): gate = jnp.dot(a, w['w_gate'], preferred_element_type=jnp.float32)  160 us
    dot_general x5, matrix products, layer(): up = jnp.dot(a, w['w_up'], preferred_element_type=jnp.float32)  156 us
    dot_general x5, matrix products, matmul(): jnp.dot(a, w, preferred_element_type=jnp.float32).astype(jnp.bfloat16)  135 us
    psum x1, blocking collectives, step(): squares = lax.psum(sum((jnp.sum(g * g) for g in gradients)), 's')  63.4 us
    psum x1, waiting for transfers between devices, summed(): lax.psum(lax.psum_scatter(term, 's', scatter_dimension=0, tiled=True), 'r')  56.3 us
  transfers between devices with their start and end apart: 13, of which 12 were waited for; matrix products, arithmetic and copies ran while one was open for 29% of the time, Pallas kernels for 0%

commit v1 on v0

v1 whole, which is shorter than its diff:
```python
import jax
import jax.numpy as jnp
from jax import lax
from jax.sharding import Mesh
from jax.sharding import PartitionSpec as P

F32, BF16 = jnp.float32, jnp.bfloat16
SWAP = [(0, 1), (1, 0)]


def dot(a, b, ca=1, cb=0):
    return lax.dot_general(a, b, (((ca,), (cb,)), ((), ())), preferred_element_type=F32)


def normed(h):
    wide = h.astype(F32)
    scale = lax.rsqrt(jnp.mean(wide**2, -1, keepdims=True) + 1e-6)
    return (wide * scale).astype(BF16)


def adamw(w, m, v, g):
    m = 0.9 * m + 0.1 * g
    v = 0.95 * v + 0.05 * g * g
    step = m * lax.rsqrt(v + 1e-8) + 0.1 * w
    return (w - 0.02 * step).astype(BF16), m, v


def solution(mesh):
    reps, groups, shards = (mesh.shape[a] for a in ("rep", "r", "s"))
    chips = shards // 2
    fine = Mesh(mesh.devices.reshape(reps, groups, chips, 2), ("rep", "r", "q", "c"))
    to_half = [(s, 2 * (s % chips) + s // chips) for s in range(shards)]
    from_half = [(b, a) for a, b in to_half]
    near = [(i, i ^ 1) for i in range(groups)]
    wrap = [(i, groups - 1 - i) for i in range(groups)]

    def step(x, dy, *arrays):
        weights, m, v = (arrays[i : i + 3] for i in (0, 3, 6))
        layers = weights[0].shape[0]
        first = lax.axis_index("c") == 0

        def columns(w):
            low, high = jnp.split(w, 2, axis=-1)
            keep, send = jnp.where(first, low, high), jnp.where(first, high, low)
            came = lax.ppermute(send, "c", SWAP)
            return jnp.concatenate([jnp.where(first, keep, came), jnp.where(first, came, keep)], 0)

        def fetched(name, number):
            w = weights[name][number]
            part = lax.ppermute(w, ("q", "c"), to_half) if name == 2 else columns(w)
            mine = lax.all_gather(part, "q", axis=0, tiled=True)
            return mine, lax.ppermute(mine, "c", SWAP)

        def summed(name, mine, other):
            half = (mine + lax.ppermute(other, "c", SWAP).astype(F32)).astype(BF16)
            part = lax.psum_scatter(half, "q", scatter_dimension=0, tiled=True)
            if name == 2:
                block = lax.ppermute(part, ("q", "c"), from_half)
            else:
                low, high = jnp.split(part, 2, axis=0)
                keep, send = jnp.where(first, low, high), jnp.where(first, high, low)
                came = lax.ppermute(send, "c", SWAP)
                block = jnp.concatenate([jnp.where(first, keep, came), jnp.where(first, came, keep)], 1)
            pieces = []
            for piece, ways in zip(jnp.split(block, 2, axis=1), ((near, wrap), (wrap, near)), strict=True):
                for way in ways:
                    piece = (piece.astype(F32) + lax.ppermute(piece, "r", way).astype(F32)).astype(BF16)
                pieces.append(piece)
            return jnp.concatenate(pieces, 1)

        full = [[fetched(name, number) for name in range(3)] for number in range(layers)]
        h, kept = x[0], []
        for number in range(layers):
            a, back = jax.vjp(normed, h)
            gates = [dot(a, w) for w in full[number][0]]
            ups = [dot(a, w) for w in full[number][1]]
            acts = [(jax.nn.silu(g) * u).astype(BF16) for g, u in zip(gates, ups, strict=True)]
            kept.append((a, back, gates, ups, acts))
            if number < layers - 1:
                h = h + sum(dot(t, w) for t, w in zip(acts, full[number][2], strict=True)).astype(BF16)

        by_h, blocks = dy[0], [[None] * layers for _ in range(3)]
        for number in reversed(range(layers)):
            a, back, gates, ups, acts = kept[number]
            blocks[2][number] = summed(2, dot(acts[0], by_h, 0, 0), dot(acts[1], by_h, 0, 0).astype(BF16))
            by_gate, by_up = [None] * 2, [None] * 2
            for i in (1, 0):
                by_act = dot(by_h, full[number][2][i], 1, 1).astype(BF16).astype(F32)
                on = jax.nn.sigmoid(gates[i])
                by_up[i] = (by_act * (gates[i] * on)).astype(BF16)
                by_gate[i] = (by_act * ups[i] * (on * (1.0 + gates[i] * (1.0 - on)))).astype(BF16)
            for name, by in ((0, by_gate), (1, by_up)):
                blocks[name][number] = summed(name, dot(a, by[0], 0, 0), dot(a, by[1], 0, 0).astype(BF16))
            if number > 0:
                by_a = [sum(dot(t, w, 1, 1) for t, w in zip(by, full[number][name], strict=True)).astype(BF16) for name, by in ((0, by_gate), (1, by_up))]
                by_h = by_h + back(by_a[0] + by_a[1])[0]

        gradients = [jnp.stack(b).astype(F32) for b in blocks]
        squares = lax.psum(sum(jnp.sum(g * g) for g in gradients), ("r", "q", "c")) / groups
        count = shards * sum(g.size for g in gradients)
        factor = jnp.minimum(1.0, 0.5 * lax.rsqrt(squares / count + 1e-30))
        new = [adamw(w.astype(F32), m, v, g * factor) for w, m, v, g in zip(weights, m, v, gradients, strict=True)]
        return tuple(one[which] for which in range(3) for one in new)

    states, cut = P(("rep", "r", "q", "c"), None, None), P(None, ("q", "c"), None)
    return jax.shard_map(
        step,
        mesh=fine,
        in_specs=(states, states) + (cut,) * 9,
        out_specs=(P("rep", ("q", "c"), None),) * 9,
        check_vma=False,
    )
```

time: 1230 us -> 1270 us (1.033)
  waiting for transfers between devices: 633 us -> 534 us
  matrix products: 451 us -> 527 us
  starting transfers between devices: 0.53 us -> 59.4 us
    reduce_scatter x6, waiting for transfers between devices: 401 us -> 241 us  [summed(): part = lax.psum_scatter(half, 'q', scatter_dimension=0, tiled=True)]
    dot_general x15 -> x30, matrix products: 451 us -> 527 us  [dot(): lax.dot_general(a, b, (((ca,), (cb,)), ((), ())), preferred_element_type=...]
    all_gather x6, waiting for transfers between devices: 174 us -> 240 us  [fetched(): mine = lax.all_gather(part, 'q', axis=0, tiled=True)]
    ppermute x0 -> x48, starting transfers between devices: none -> 58.9 us  [the longest x24 23.2 us: summed(): lax.ppermute(piece, 'r', way).astype(F32)]
    psum x1 -> x0, waiting for transfers between devices: 56.3 us -> none  [summed(): lax.psum(lax.psum_scatter(term, 's', scatter_dimension=0, tiled=True), 'r')]
    ppermute x0 -> x48, waiting for transfers between devices: none -> 52.4 us  [the longest x2 18.4 us: fetched(): part = lax.ppermute(w, ('q', 'c'), to_half) if name == 2 else columns(w)]
  transfers between devices with their start and end apart: 13 -> 60, of which waited for: 12 -> 27; matrix products, arithmetic and copies ran while one was open for 29% -> 41% of each run, Pallas kernels for 0% -> 0%
where the time goes in v1:
time: 1270 us
  waiting for transfers between devices  534 us (42%)
  matrix products  527 us (41%)
  blocking collectives  69.4 us (5%)
  starting transfers between devices  59.4 us (5%)
  other arithmetic  41.6 us (3%)
  local copies, waits for them, and re-layouts  19.7 us (2%)
  between operations  17.8 us (1%)
    dot_general x30, matrix products, dot(): lax.dot_general(a, b, (((ca,), (cb,)), ((), ())), preferred_element_type=...  527 us
    reduce_scatter x6, waiting for transfers between devices, summed(): part = lax.psum_scatter(half, 'q', scatter_dimension=0, tiled=True)  241 us
    all_gather x6, waiting for transfers between devices, fetched(): mine = lax.all_gather(part, 'q', axis=0, tiled=True)  240 us
    psum x1, blocking collectives, step(): lax.psum(sum((jnp.sum(g * g) for g in gradients)), ('r', 'q', 'c')) / groups  69.4 us
  transfers between devices with their start and end apart: 60, of which 27 were waited for; matrix products, arithmetic and copies ran while one was open for 41% of the time, Pallas kernels for 0%

profile of v1, /device:TPU:1, one launch (start us, length us, event | category | flops | bytes accessed | tf_op | source)
XLA Modules:
  0.0 1268.8 jit_solution(10099034451827583113)
XLA Ops:
  72.2 54.5 %all-gather.15.cloned.1.call-done = bf16[1280,1792]{1,0:T(8,128)(2,1)} async-done(((bf16[80,1792]{1,0:T(8,128)(2,1)}), bf16[1280,1792]{1,0:T(8,128)(2,1)}) %all-gather.15.cloned.1.call-update) | async-done | bytes 4587536 | tf_op jit(solution)/shard_map/all_gather | solution.py:51
  127.6 54.5 %all-gather.17.cloned.1.call-done = bf16[1280,1792]{1,0:T(8,128)(2,1)} async-done(((bf16[80,1792]{1,0:T(8,128)(2,1)}), bf16[1280,1792]{1,0:T(8,128)(2,1)}) %all-gather.17.cloned.1.call-update) | async-done | bytes 4587536 | tf_op jit(solution)/shard_map/all_gather | solution.py:51
  183.0 54.3 %all-gather.9.cloned.1.call-done = bf16[1280,1792]{1,0:T(8,128)(2,1)} async-done(((bf16[80,1792]{1,0:T(8,128)(2,1)}), bf16[1280,1792]{1,0:T(8,128)(2,1)}) %all-gather.9.cloned.1.call-update) | async-done | bytes 4587536 | tf_op jit(solution)/shard_map/all_gather | solution.py:51
  254.5 21.1 %multiply_convert_fusion.3 = (bf16[2048,1792]{1,0:T(8,128)(2,1)}, f32[2048,1792]{1,0:T(8,128)}) fusion(f32[2048,1792]{1,0:T(8,128)} %fusion.94, bf16[1280,1792]{1,0:T(8,128)(2,1)} %all-gather.11.cloned.1.call-done, bf16[1,2048,1280]{1,2,0:T(8,128)(2,1)} %copy.20, f32[2048]{0:T(1024)S(1)} %add_rsqrt_fusion), kind=kOutput, calls=%fused_computation.33 | convolution fusion | flops 9425125376 | bytes 46538752 | tf_op jit(solution)/shard_map/dot_general | solution.py:12
  275.6 17.0 %all-gather.13.cloned.1.call-done = bf16[1792,1280]{1,0:T(8,128)(2,1)} async-done(((bf16[112,1280]{1,0:T(8,128)(2,1)}), bf16[1792,1280]{1,0:T(8,128)(2,1)}) %all-gather.13.cloned.1.call-update) | async-done | bytes 4587536 | tf_op jit(solution)/shard_map/all_gather | solution.py:51
  293.5 54.3 %all-gather.7.cloned.1.call-done = bf16[1792,1280]{1,0:T(8,128)(2,1)} async-done(((bf16[112,1280]{1,0:T(8,128)(2,1)}), bf16[1792,1280]{1,0:T(8,128)(2,1)}) %all-gather.7.cloned.1.call-update) | async-done | bytes 4587536 | tf_op jit(solution)/shard_map/all_gather | solution.py:51
  365.0 21.0 %multiply_convert_fusion.2 = (bf16[2048,1792]{1,0:T(8,128)(2,1)}, f32[2048,1792]{1,0:T(8,128)}) fusion(f32[2048,1792]{1,0:T(8,128)} %fusion.90, bf16[1280,1792]{1,0:T(8,128)(2,1)} %collective-permute-done.5, bf16[1,2048,1280]{1,2,0:T(8,128)(2,1)} %copy.20, f32[2048]{0:T(1024)S(1)} %add_rsqrt_fusion), kind=kOutput, calls=%fused_computation.30 | convolution fusion | flops 9425125376 | bytes 46538752 | tf_op jit(solution)/shard_map/dot_general | solution.py:12
  402.3 19.8 %fusion.20 = (f32[2048]{0:T(1024)S(1)}, bf16[2048,1280]{0,1:T(8,128)(2,1)}) fusion(f32[2048,1280]{0,1:T(8,128)} %fusion.111, bf16[2048,1792]{1,0:T(8,128)(2,1)} %get-tuple-element.54, bf16[1792,1280]{1,0:T(8,128)(2,1)} %all-gather.13.cloned.1.call-done, bf16[1,2048,1280]{1,2,0:T(8,128)(2,1)} %copy.20), kind=kOutput, calls=%fused_computation.43 | convolution fusion | flops 9410967552 | bytes 32907264 | tf_op jit(solution)/shard_map/dot_general | solution.py:12
  422.2 16.4 %fusion.74 = f32[2048,1792]{1,0:T(8,128)} fusion(bf16[1280,1792]{1,0:T(8,128)(2,1)} %collective-permute-done.10, bf16[2048,1280]{0,1:T(8,128)(2,1)} %get-tuple-element.57, f32[2048]{0:T(1024)S(1)} %fusion.96), kind=kOutput, calls=%fused_computation.114 | convolution fusion | flops 9403105280 | bytes 24518656 | tf_op jit(solution)/shard_map/dot_general | solution.py:12
  453.8 24.4 %fusion.5 = (bf16[2048,1792]{1,0:T(8,128)(2,1)}, bf16[2048,1792]{1,0:T(8,128)(2,1)}) fusion(f32[2048,1792]{1,0:T(8,128)} %fusion.72, f32[2048,1792]{1,0:T(8,128)} %fusion.74, bf16[1792,1280]{1,0:T(8,128)(2,1)} %collective-permute-done.9, bf16[1,2048,1280]{2,1,0:T(8,128)(2,1)} %param.12), kind=kOutput, calls=%fused_computation.17 | convolution fusion | flops 9450291200 | bytes 53870592 | tf_op jit(solution)/shard_map/dot_general | solution.py:12
  507.5 16.3 %fusion.113 = f32[2048,1280]{0,1:T(8,128)} fusion(bf16[2048,1792]{1,0:T(8,128)(2,1)} %get-tuple-element.20, bf16[1280,1792]{1,0:T(8,128)(2,1)} %collective-permute-done.10), kind=kOutput, calls=%fused_computation.210 | convolution fusion | flops 9395240960 | bytes 22413312 | tf_op jit(solution)/shard_map/dot_general | solution.py:12
  550.2 24.1 %fusion.2 = (bf16[2048,1792]{1,0:T(8,128)(2,1)}, bf16[2048,1792]{1,0:T(8,128)(2,1)}) fusion(f32[2048,1792]{1,0:T(8,128)} %fusion.76, f32[2048,1792]{1,0:T(8,128)} %fusion.78, bf16[1792,1280]{1,0:T(8,128)(2,1)} %all-gather.7.cloned.1.call-done, bf16[1,2048,1280]{2,1,0:T(8,128)(2,1)} %param.12), kind=kOutput, calls=%fused_computation.14 | convolution fusion | flops 9450291200 | bytes 53870592 | tf_op jit(solution)/shard_map/dot_general | solution.py:12
  574.3 16.7 %add_convert_fusion = bf16[2048,1280]{0,1:T(8,128)(2,1)} fusion(f32[2048,1280]{0,1:T(8,128)} %fusion.113, bf16[2048,1792]{1,0:T(8,128)(2,1)} %get-tuple-element.18, bf16[1280,1792]{1,0:T(8,128)(2,1)} %all-gather.15.cloned.1.call-done), kind=kOutput, calls=%fused_computation.46 | convolution fusion | flops 9400483840 | bytes 27656192 | tf_op jit(solution)/shard_map/dot_general | solution.py:12
  606.9 19.5 %fusion.22 = (f32[2048]{0:T(1024)S(1)}, bf16[2048,1280]{0,1:T(8,128)(2,1)}) fusion(bf16[2048,1280]{0,1:T(8,128)(2,1)} %get-tuple-element.57, bf16[2048,1280]{0,1:T(8,128)(2,1)} %add_convert_fusion, f32[2048,1280]{0,1:T(8,128)} %fusion.112, bf16[2048,1792]{1,0:T(8,128)(2,1)} %get-tuple-element.19, bf16[1280,1792]{1,0:T(8,128)(2,1)} %all-gather.17.cloned.1.call-done), kind=kOutput, calls=%fused_computation.45 | convolution fusion | flops 9413588992 | bytes 38150144 | tf_op jit(solution)/shard_map/dot_general | solution.py:12
  669.0 17.2 %convolution_convert_fusion.1 = bf16[1280,1792]{1,0:T(8,128)(2,1)} fusion(bf16[2048,1792]{1,0:T(8,128)(2,1)} %convolution_convert_fusion.4, f32[2048,1792]{1,0:T(8,128)} %fusion.90, bf16[1,2048,1280]{1,2,0:T(8,128)(2,1)S(1)} %bitcast.93, f32[2048]{0:T(1024)S(1)} %copy-done.12), kind=kOutput, calls=%fused_computation.56 | convolution fusion | flops 9431089152 | bytes 31858688 | tf_op jit(solution)/shard_map/dot_general | solution.py:12
  702.4 22.0 %convolution_convert_fusion.3 = bf16[1280,1792]{1,0:T(8,128)(2,1)} fusion(f32[2048,1792]{1,0:T(8,128)} %get-tuple-element.53, bf16[2048,1792]{1,0:T(8,128)(2,1)} %convolution_convert_fusion.4, f32[2048,1792]{1,0:T(8,128)} %fusion.90, bf16[1,2048,1280]{1,2,0:T(8,128)(2,1)} %copy.20, f32[2048]{0:T(1024)S(1)} %copy-done.12), kind=kOutput, calls=%fused_computation.58 | convolution fusion | flops 9445769216 | bytes 46538752 | tf_op jit(solution)/shard_map/dot_general | solution.py:12
  739.9 21.5 %add_convert_fusion.6 = bf16[1280,1792]{1,0:T(8,128)(2,1)} fusion(bf16[1280,1792]{1,0:T(8,128)(2,1)} %collective-permute-done.24, bf16[2048,1792]{1,0:T(8,128)(2,1)} %convolution_convert_fusion.5, f32[2048,1792]{1,0:T(8,128)} %fusion.94, bf16[1,2048,1280]{1,2,0:T(8,128)(2,1)} %copy.20, f32[2048]{0:T(1024)S(1)} %copy-done.12), kind=kOutput, calls=%fused_computation.52 | convolution fusion | flops 9435676672 | bytes 36446208 | tf_op jit(solution)/shard_map/dot_general | solution.py:12
  761.5 22.3 %add_convert_fusion.8 = bf16[1280,1792]{1,0:T(8,128)(2,1)} fusion(bf16[1280,1792]{1,0:T(8,128)(2,1)} %collective-permute-done.12, f32[2048,1792]{1,0:T(8,128)} %get-tuple-element.55, bf16[2048,1792]{1,0:T(8,128)(2,1)} %convolution_convert_fusion.5, f32[2048,1792]{1,0:T(8,128)} %fusion.94, bf16[1,2048,1280]{1,2,0:T(8,128)(2,1)} %copy.20, f32[2048]{0:T(1024)S(1)} %copy-done.12), kind=kOutput, calls=%fused_computation.54 | convolution fusion | flops 9450356736 | bytes 51126272 | tf_op jit(solution)/shard_map/dot_general | solution.py:12
  783.9 18.0 %convolution_convert_fusion.8 = bf16[1792,1280]{1,0:T(8,128)(2,1)S(1)} fusion(f32[2048,1792]{1,0:T(8,128)} %fusion.74, bf16[1,2048,1280]{2,1,0:T(8,128)(2,1)} %param.12, f32[2048,1792]{1,0:T(8,128)} %fusion.72), kind=kOutput, calls=%fused_computation.63 | convolution fusion | flops 9419554816 | bytes 39190528 | tf_op jit(solution)/shard_map/dot_general | solution.py:12
  809.7 22.5 %add_convert_fusion.3 = bf16[1792,1280]{1,0:T(8,128)(2,1)} fusion(bf16[1792,1280]{1,0:T(8,128)(2,1)} %collective-permute-done.42, f32[2048,1792]{1,0:T(8,128)} %fusion.78, bf16[1,2048,1280]{2,1,0:T(8,128)(2,1)} %param.12, f32[2048,1792]{1,0:T(8,128)} %fusion.76), kind=kOutput, calls=%fused_computation.49 | convolution fusion | flops 9424142336 | bytes 43778048 | tf_op jit(solution)/shard_map/dot_general | solution.py:12
  885.0 77.7 %reduce-scatter.7.cloned.1.call-done = bf16[80,1792]{1,0:T(8,128)(2,1)} async-done(((bf16[1280,1792]{1,0:T(8,128)(2,1)}), bf16[80,1792]{1,0:T(8,128)(2,1)}) %reduce-scatter.7.cloned.1.call-update) | async-done | bytes 286736 | tf_op jit(solution)/shard_map/reduce_scatter | solution.py:56
  966.4 78.0 %reduce-scatter.17.cloned.1.call-done = bf16[112,1280]{1,0:T(8,128)(2,1)} async-done(((bf16[1792,1280]{1,0:T(8,128)(2,1)}), bf16[112,1280]{1,0:T(8,128)(2,1)}) %reduce-scatter.17.cloned.1.call-update) | async-done | bytes 286736 | tf_op jit(solution)/shard_map/reduce_scatter | solution.py:56
  1051.1 74.9 %reduce-scatter.15.cloned.1.call-done = bf16[112,1280]{1,0:T(8,128)(2,1)} async-done(((bf16[1792,1280]{1,0:T(8,128)(2,1)}), bf16[112,1280]{1,0:T(8,128)(2,1)}) %reduce-scatter.15.cloned.1.call-update) | async-done | bytes 286736 | tf_op jit(solution)/shard_map/reduce_scatter | solution.py:56
  1182.6 69.4 %psum.7 = f32[]{:T(128)} all-reduce(f32[]{:T(128)S(6)} %add.264), channel_id=1, replica_groups=mesh['rep'=1,'r'=4,'q'=16,'c'=2] {'r','q','c'}, use_global_device_ids=true, to_apply=%region_12.13 | all-reduce | flops 1 | bytes 8 | tf_op jit(solution)/shard_map/psum | solution.py:99
  (257 shorter events, 413.4 us)
Async XLA Ops:
  11.6 115.1 %all-gather.15.cloned.1.call-start = ((), (), s32[]{:S(2)}) async-start(), calls=%async_computation.10 | async-start | bytes 4874240 | tf_op jit(solution)/shard_map/all_gather | solution.py:51
  13.9 168.2 %all-gather.17.cloned.1.call-start = ((), (), s32[]{:S(2)}) async-start(), calls=%async_computation.11 | async-start | bytes 4874240 | tf_op jit(solution)/shard_map/all_gather | solution.py:51
  17.3 220.0 %all-gather.9.cloned.1.call-start = ((), (), s32[]{:S(2)}) async-start(), calls=%async_computation.7 | async-start | bytes 4874240 | tf_op jit(solution)/shard_map/all_gather | solution.py:51
  19.7 272.9 %all-gather.13.cloned.1.call-start = ((), (), s32[]{:S(2)}) async-start(), calls=%async_computation.9 | async-start | bytes 4874240 | tf_op jit(solution)/shard_map/all_gather | solution.py:51
  34.7 313.1 %all-gather.7.cloned.1.call-start = ((), (), s32[]{:S(2)}) async-start(), calls=%async_computation.6 | async-start | bytes 4874240 | tf_op jit(solution)/shard_map/all_gather | solution.py:51
  45.7 823.1 %reduce-scatter.13.cloned.1.call-start = ((), (), s32[]{:S(2)}) async-start(), calls=%async_computation.15 | async-start | bytes 4874240 | tf_op jit(solution)/shard_map/reduce_scatter | solution.py:56
  71.0 294.0 %collective-permute-start.5 = (bf16[1280,1792]{1,0:T(8,128)(2,1)}, bf16[1280,1792]{1,0:T(8,128)(2,1)}, u32[]{:S(2)}, u32[]{:S(2)}) collective-permute-start(bf16[1280,1792]{1,0:T(8,128)(2,1)} %all-gather.11.cloned.1.call-done), channel_id=1, source_target_pairs={{0,1},{1,0},{2,3},{3,2},{4,5},{5,4},{6,7},{7,6},{8,9},{9,8},{10,11... | collective-permute-start | bytes 13762568 | tf_op jit(solution)/shard_map/ppermute | solution.py:52
  126.7 295.4 %collective-permute-start.10 = (bf16[1280,1792]{1,0:T(8,128)(2,1)}, bf16[1280,1792]{1,0:T(8,128)(2,1)}, u32[]{:S(2)}, u32[]{:S(2)}) collective-permute-start(bf16[1280,1792]{1,0:T(8,128)(2,1)} %all-gather.15.cloned.1.call-done), channel_id=1, source_target_pairs={{0,1},{1,0},{2,3},{3,2},{4,5},{5,4},{6,7},{7,6},{8,9},{9,8},{10,11... | collective-permute-start | bytes 13762568 | tf_op jit(solution)/shard_map/ppermute | solution.py:52
  182.1 256.4 %collective-permute-start.11 = (bf16[1280,1792]{1,0:T(8,128)(2,1)}, bf16[1280,1792]{1,0:T(8,128)(2,1)}, u32[]{:S(2)}, u32[]{:S(2)}) collective-permute-start(bf16[1280,1792]{1,0:T(8,128)(2,1)} %all-gather.17.cloned.1.call-done), channel_id=1, source_target_pairs={{0,1},{1,0},{2,3},{3,2},{4,5},{5,4},{6,7},{7,6},{8,9},{9,8},{10,11... | collective-permute-start | bytes 13762568 | tf_op jit(solution)/shard_map/ppermute | solution.py:52
  237.4 110.5 %collective-permute-start.4 = (bf16[1280,1792]{1,0:T(8,128)(2,1)}, bf16[1280,1792]{1,0:T(8,128)(2,1)}, u32[]{:S(2)}, u32[]{:S(2)}) collective-permute-start(bf16[1280,1792]{1,0:T(8,128)(2,1)} %all-gather.9.cloned.1.call-done), channel_id=1, source_target_pairs={{0,1},{1,0},{2,3},{3,2},{4,5},{5,4},{6,7},{7,6},{8,9},{9,8},{10,11... | collective-permute-start | bytes 13762568 | tf_op jit(solution)/shard_map/ppermute | solution.py:52
  292.6 93.5 %collective-permute-start.6 = (bf16[1792,1280]{1,0:T(8,128)(2,1)}, bf16[1792,1280]{1,0:T(8,128)(2,1)}, u32[]{:S(2)}, u32[]{:S(2)}) collective-permute-start(bf16[1792,1280]{1,0:T(8,128)(2,1)} %all-gather.13.cloned.1.call-done), channel_id=1, source_target_pairs={{0,1},{1,0},{2,3},{3,2},{4,5},{5,4},{6,7},{7,6},{8,9},{9,8},{10,11... | collective-permute-start | bytes 13762568 | tf_op jit(solution)/shard_map/ppermute | solution.py:52
  347.9 106.0 %collective-permute-start.9 = (bf16[1792,1280]{1,0:T(8,128)(2,1)}, bf16[1792,1280]{1,0:T(8,128)(2,1)}, u32[]{:S(2)}, u32[]{:S(2)}) collective-permute-start(bf16[1792,1280]{1,0:T(8,128)(2,1)} %all-gather.7.cloned.1.call-done), channel_id=1, source_target_pairs={{0,1},{1,0},{2,3},{3,2},{4,5},{5,4},{6,7},{7,6},{8,9},{9,8},{10,11... | collective-permute-start | bytes 13762568 | tf_op jit(solution)/shard_map/ppermute | solution.py:52
  507.0 179.2 %collective-permute-start.18 = (bf16[1280,1792]{1,0:T(8,128)(2,1)}, bf16[1280,1792]{1,0:T(8,128)(2,1)}, u32[]{:S(2)}, u32[]{:S(2)}) collective-permute-start(bf16[1280,1792]{1,0:T(8,128)(2,1)} %convolution_convert_fusion.2), channel_id=1, source_target_pairs={{0,1},{1,0},{2,3},{3,2},{4,5},{5,4},{6,7},{7,6},{8,9},{9,8},{10,11... | collective-permute-start | bytes 13762568 | tf_op jit(solution)/shard_map/ppermute | solution.py:55
  507.0 119.4 %collective-permute-start.30 = (bf16[1280,1792]{1,0:T(8,128)(2,1)}, bf16[1280,1792]{1,0:T(8,128)(2,1)}, u32[]{:S(2)}, u32[]{:S(2)}) collective-permute-start(bf16[1280,1792]{1,0:T(8,128)(2,1)} %convolution_convert_fusion), channel_id=1, source_target_pairs={{0,1},{1,0},{2,3},{3,2},{4,5},{5,4},{6,7},{7,6},{8,9},{9,8},{10,11... | collective-permute-start | bytes 13762568 | tf_op jit(solution)/shard_map/ppermute | solution.py:55
  641.4 228.7 %reduce-scatter.9.cloned.1.call-start = ((), (), s32[]{:S(2)}) async-start(), calls=%async_computation.13 | async-start | bytes 4874240 | tf_op jit(solution)/shard_map/reduce_scatter | solution.py:56
  702.4 179.0 %reduce-scatter.11.cloned.1.call-start = ((), (), s32[]{:S(2)}) async-start(), calls=%async_computation.14 | async-start | bytes 4874240 | tf_op jit(solution)/shard_map/reduce_scatter | solution.py:56
  761.4 201.3 %reduce-scatter.7.cloned.1.call-start = ((), (), s32[]{:S(2)}) async-start(), calls=%async_computation.12 | async-start | bytes 4874240 | tf_op jit(solution)/shard_map/reduce_scatter | solution.py:56
  783.9 260.6 %reduce-scatter.17.cloned.1.call-start = ((), (), s32[]{:S(2)}) async-start(), calls=%async_computation.17 | async-start | bytes 4874240 | tf_op jit(solution)/shard_map/reduce_scatter | solution.py:56
  832.2 293.8 %reduce-scatter.15.cloned.1.call-start = ((), (), s32[]{:S(2)}) async-start(), calls=%async_computation.16 | async-start | bytes 4874240 | tf_op jit(solution)/shard_map/reduce_scatter | solution.py:56
  869.8 256.2 %collective-permute-start.31 = (bf16[40,1792]{1,0:T(8,128)(2,1)S(1)}, bf16[40,1792]{1,0:T(8,128)(2,1)S(1)}, u32[]{:S(2)}, u32[]{:S(2)}) collective-permute-start(bf16[40,1792]{1,0:T(8,128)(2,1)S(1)} %broadcast_select_fusion.2), channel_id=1, source_target_pairs={{0,1},{1,0},{2,3},{3,2},{4,5},{5,4},{6,7},{7,6},{8,9},{9,8},{10,11... | collective-permute-start | bytes 430088 | tf_op jit(solution)/shard_map/ppermute | solution.py:62
  871.1 262.7 %collective-permute-start.19 = (bf16[40,1792]{1,0:T(8,128)(2,1)S(1)}, bf16[40,1792]{1,0:T(8,128)(2,1)S(1)}, u32[]{:S(2)}, u32[]{:S(2)}) collective-permute-start(bf16[40,1792]{1,0:T(8,128)(2,1)S(1)} %broadcast_select_fusion.10), channel_id=1, source_target_pairs={{0,1},{1,0},{2,3},{3,2},{4,5},{5,4},{6,7},{7,6},{8,9},{9,8},{10,11... | collective-permute-start | bytes 430088 | tf_op jit(solution)/shard_map/ppermute | solution.py:62
  882.3 253.7 %collective-permute-start.25 = (bf16[40,1792]{1,0:T(8,128)(2,1)S(1)}, bf16[40,1792]{1,0:T(8,128)(2,1)S(1)}, u32[]{:S(2)}, u32[]{:S(2)}) collective-permute-start(bf16[40,1792]{1,0:T(8,128)(2,1)S(1)} %broadcast_select_fusion.6), channel_id=1, source_target_pairs={{0,1},{1,0},{2,3},{3,2},{4,5},{5,4},{6,7},{7,6},{8,9},{9,8},{10,11... | collective-permute-start | bytes 430088 | tf_op jit(solution)/shard_map/ppermute | solution.py:62
  963.7 175.2 %collective-permute-start.13 = (bf16[40,1792]{1,0:T(8,128)(2,1)S(1)}, bf16[40,1792]{1,0:T(8,128)(2,1)S(1)}, u32[]{:S(2)}, u32[]{:S(2)}) collective-permute-start(bf16[40,1792]{1,0:T(8,128)(2,1)S(1)} %broadcast_select_fusion.14), channel_id=1, source_target_pairs={{0,1},{1,0},{2,3},{3,2},{4,5},{5,4},{6,7},{7,6},{8,9},{9,8},{10,11... | collective-permute-start | bytes 430088 | tf_op jit(solution)/shard_map/ppermute | solution.py:62
  1044.5 110.7 %collective-permute-start.43 = (bf16[112,1280]{1,0:T(8,128)(2,1)}, bf16[112,1280]{1,0:T(8,128)(2,1)S(1)}, u32[]{:S(2)}, u32[]{:S(2)}) collective-permute-start(bf16[112,1280]{1,0:T(8,128)(2,1)} %reduce-scatter.17.cloned.1.call-done), channel_id=1, source_target_pairs={{0,0},{2,1},{4,2},{6,3},{8,4},{10,5},{12,6},{14,7},{16,8},{18,9},{... | collective-permute-start | bytes 860168 | tf_op jit(solution)/shard_map/ppermute | solution.py:58
  (60 other events, 1343.5 us)
Sparse Core Ops, SparseCore 0:
  11.8 59.2 all-gather.10
  73.8 52.8 all-gather.14
  129.5 52.5 all-gather.16
  184.7 52.5 all-gather.8
  240.0 52.5 all-gather.12
  295.2 52.5 all-gather.6
  641.5 76.3 reduce-scatter.12
  721.2 78.3 reduce-scatter.8
  803.0 78.3 reduce-scatter.10
  884.5 78.1 reduce-scatter.6
  966.1 78.3 reduce-scatter.16
  1047.7 78.3 reduce-scatter.14

commit v2 on v0

v2 whole, which is shorter than its diff:
```python
import functools

import jax
import jax.numpy as jnp
from jax import lax
from jax.experimental import pallas as pl
from jax.experimental.pallas import tpu as pltpu
from jax.sharding import Mesh
from jax.sharding import PartitionSpec as P

F32, BF16 = jnp.float32, jnp.bfloat16
MESH = pl.DeviceIdType.MESH
SWAP = [(0, 1), (1, 0)]
NAMES = ("w_gate", "w_up", "w_down")
TILE = 256
SIDE = 4


def matmul(a, w):
    return jnp.dot(a, w, preferred_element_type=F32).astype(BF16)


def normed(h):
    wide = h.astype(F32)
    scale = lax.rsqrt(jnp.mean(wide**2, -1, keepdims=True) + 1e-6)
    return (wide * scale).astype(BF16)


def adamw(w, m, v, g):
    m = 0.9 * m + 0.1 * g
    v = 0.95 * v + 0.05 * g * g
    step = m * lax.rsqrt(v + 1e-8) + 0.1 * w
    return (w - 0.02 * step).astype(BF16), m, v


def near(x):
    return x + 1 - 2 * lax.rem(x, 2)


def wrap(x):
    return SIDE - 1 - x


def upper(rows):
    return (rows // 16 + 1) // 2 * 16


class Host:
    pass


def gradient_call(number, product=None, scatter=None, across=None):
    operands, in_specs, out_shapes, out_specs, scratch = [], [], [], [], []
    names_in, names_out, names_scratch = [], [], []
    anywhere, vmem = pl.BlockSpec(memory_space=pl.ANY), pl.BlockSpec(memory_space=pltpu.VMEM)
    dma = pltpu.SemaphoreType.DMA

    def take(name, value, spec):
        operands.append(value), in_specs.append(spec), names_in.append(name)

    def give(name, shape, dtype, spec):
        out_shapes.append(jax.ShapeDtypeStruct(shape, dtype)), out_specs.append(spec), names_out.append(name)

    def hold(name, what):
        scratch.append(what), names_scratch.append(name)

    steps, tiles, flops, moved = 1, 0, 0, 0
    if product:
        kind, resident, streamed = product
        tokens, half = streamed.shape[0], streamed.shape[1] // 2
        tiles = half // TILE
        d = resident.shape[0] if kind == "columns" else resident.shape[1]
        tile = (d, TILE) if kind == "columns" else (TILE, d)

        def place(i):
            n = jnp.clip(i - tiles, 0, tiles - 1)
            return (0, n) if kind == "columns" else (n, 0)

        whole = (d, half) if kind == "columns" else (half, d)
        take("resident", resident, vmem)
        take("streamed", streamed, anywhere)
        give("wide", whole, F32, pl.BlockSpec(tile, place))
        give("narrow", whole, BF16, pl.BlockSpec(tile, place))
        hold("stream", pltpu.VMEM((2, tokens, TILE), BF16))
        hold("stream_sem", dma((2,)))
        hold("sent", pltpu.VMEM((tiles, *tile), BF16))
        hold("came", pltpu.VMEM((tiles, *tile), BF16))
        hold("pair_send", dma((tiles,)))
        hold("pair_recv", dma((tiles,)))
        steps = max(steps, 2 * tiles)
        flops += 4 * tokens * half * d
        moved += streamed.size * 2 + resident.size * 2 + 6 * d * half
    if scatter:
        wide, narrow = scatter
        rows, columns = wide.shape[2:]
        part = columns // 2
        cut = upper(rows)
        take("wide_in", wide, anywhere)
        take("narrow_in", narrow, anywhere)
        give("block", (rows, columns), BF16, vmem)
        hold("held", pltpu.VMEM((2, 3, SIDE, rows, part), F32))
        hold("held_sem", dma((2, 3)))
        hold("got1", pltpu.VMEM((2, 2, 2, rows, part), BF16))
        hold("put2", pltpu.VMEM((2, 2, SIDE, rows, part), BF16))
        hold("got2", pltpu.VMEM((2, 2, SIDE, rows, part), BF16))
        hold("put3", pltpu.VMEM((2, rows, part), BF16))
        hold("got3", pltpu.VMEM((2, rows, part), BF16))
        hold("put4", pltpu.VMEM((2, 2, rows, part), BF16))
        hold("got4", pltpu.VMEM((2, 2, rows, part), BF16))
        hold("ring_send", dma((4, 2, 2)))
        hold("ring_recv", dma((4, 2, 2)))
        steps = max(steps, 17)
    if across is not None:
        wide_rows, wide_columns = across.shape
        take("partial", across, vmem)
        give("total", across.shape, BF16, vmem)
        hold("across_got", pltpu.VMEM((2, *across.shape), BF16))
        hold("across_put", pltpu.VMEM(across.shape, BF16))
        hold("across_send", dma((2, 2)))
        hold("across_recv", dma((2, 2)))
        steps = max(steps, 11)

    def kernel(*refs):
        k = Host()
        for name, ref in zip(names_in + names_out + names_scratch, refs, strict=True):
            setattr(k, name, ref)
        i = pl.program_id(0)
        x, q, c = lax.axis_index("r"), lax.axis_index("q"), lax.axis_index("c")
        at = (q // SIDE, lax.rem(q, SIDE))

        def beside(axis, by):
            there = lax.rem(at[axis] + by + SIDE, SIDE)
            return {"q": there * SIDE + at[1] if axis == 0 else at[0] * SIDE + there}

        peers = []
        if product:
            peers.append({"c": 1 - c})
        if scatter:
            peers += [beside(axis, by) for axis in (0, 1) for by in (1, -1)]
        if across is not None:
            peers += [{"r": near(x)}, {"r": wrap(x)}]

        def send(src, dst, send_sem, recv_sem, to):
            return pltpu.make_async_remote_copy(src_ref=src, dst_ref=dst, send_sem=send_sem, recv_sem=recv_sem, device_id=to, device_id_type=MESH)

        events = {}

        def when(step):
            def add(f):
                events.setdefault(step, []).append(f)
                return f

            return add

        @when(0)
        def _():
            barrier = pltpu.get_barrier_semaphore()
            for peer in peers:
                pl.semaphore_signal(barrier, inc=1, device_id=peer, device_id_type=MESH)
            pl.semaphore_wait(barrier, len(peers))

        if scatter:
            spans = (pl.ds(0, part), pl.ds(part, part))

            def places(p, by):
                return lax.rem(at[p] + by + SIDE, SIDE)

            def of(ref, p, by, some):
                return ref.at[places(p, by), some, :, spans[p]] if p == 0 else ref.at[some, places(p, by), :, spans[p]]

            def loads():
                return [
                    pltpu.make_async_copy(of(k.wide_in, p, by, pl.ds(0, SIDE)), k.held.at[p, n], k.held_sem.at[p, n])
                    for p in (0, 1)
                    for n, by in enumerate((0, 1, -1))
                ]

            def ring(stage):
                copies = []
                for p in (0, 1):
                    for n, by in enumerate((1, -1)):
                        if stage == 0:
                            src, dst, axis = of(k.narrow_in, p, 2, pl.ds(2 * n, 2)), k.got1.at[p, n], p
                        elif stage == 1:
                            src, dst, axis = k.put2.at[p, n], k.got2.at[p, n], p
                        elif stage == 2:
                            some = pl.ds(0, cut) if n == 0 else pl.ds(cut, rows - cut)
                            src, dst, axis = k.put3.at[p, some], k.got3.at[p, some], 1 - p
                        else:
                            src, dst, axis = k.put4.at[p, n], k.got4.at[p, n], 1 - p
                        copies.append(send(src, dst, k.ring_send.at[stage, p, n], k.ring_recv.at[stage, p, n], beside(axis, by)))
                return copies

            @when(0)
            def _():
                for copy in ring(0) + loads():
                    copy.start()

            @when(4)
            def _():
                for copy in ring(0) + loads():
                    copy.wait()
                for p in (0, 1):
                    for n in (0, 1):
                        for s in range(SIDE):
                            value = k.held[p, n + 1, s]
                            if s // 2 == n:
                                value = value + k.got1[p, n, s % 2].astype(F32)
                            k.put2[p, n, s] = value.astype(BF16)

            @when(5)
            def _():
                for copy in ring(1):
                    copy.start()

            @when(12)
            def _():
                for copy in ring(1):
                    copy.wait()
                for p in (0, 1):
                    for s in range(SIDE):
                        k.held[p, 0, s] = k.held[p, 0, s] + k.got2[p, 0, s].astype(F32) + k.got2[p, 1, s].astype(F32)
                    k.put3[p] = k.held[p, 0, places(1 - p, 2)].astype(BF16)

            @when(13)
            def _():
                for copy in ring(2):
                    copy.start()

            @when(14)
            def _():
                for copy in ring(2):
                    copy.wait()
                for p in (0, 1):
                    ahead, behind = places(1 - p, 1), places(1 - p, -1)
                    k.put4[p, 0, :cut] = (k.held[p, 0, ahead, :cut] + k.got3[p, :cut].astype(F32)).astype(BF16)
                    k.put4[p, 0, cut:] = k.held[p, 0, ahead, cut:].astype(BF16)
                    k.put4[p, 1, :cut] = k.held[p, 0, behind, :cut].astype(BF16)
                    k.put4[p, 1, cut:] = (k.held[p, 0, behind, cut:] + k.got3[p, cut:].astype(F32)).astype(BF16)

            @when(15)
            def _():
                for copy in ring(3):
                    copy.start()

            @when(16)
            def _():
                for copy in ring(3):
                    copy.wait()
                for p in (0, 1):
                    mine = k.held[p, 0, places(1 - p, 0)]
                    k.block[:, p * part : (p + 1) * part] = (mine + k.got4[p, 0].astype(F32) + k.got4[p, 1].astype(F32)).astype(BF16)

        if across is not None:
            sides = (pl.ds(0, wide_columns // 2), pl.ds(wide_columns // 2, wide_columns // 2))
            ways = ((near, wrap), (wrap, near))

            def swaps(stage):
                src = k.partial if stage == 0 else k.across_put
                return [
                    send(src.at[:, sides[p]], k.across_got.at[stage, :, sides[p]], k.across_send.at[stage, p], k.across_recv.at[stage, p], {"r": ways[p][stage](x)})
                    for p in (0, 1)
                ]

            @when(0)
            def _():
                for copy in swaps(0):
                    copy.start()

            @when(4)
            def _():
                for copy in swaps(0):
                    copy.wait()
                k.across_put[...] = (k.partial[...].astype(F32) + k.across_got[0].astype(F32)).astype(BF16)

            @when(5)
            def _():
                for copy in swaps(1):
                    copy.start()

            @when(10)
            def _():
                for copy in swaps(1):
                    copy.wait()
                k.total[...] = (k.across_put[...].astype(F32) + k.across_got[1].astype(F32)).astype(BF16)

        if product:

            def fetch(n):
                theirs = (n < tiles).astype(jnp.int32)
                which = theirs * (1 - c) + (1 - theirs) * c
                column = pl.multiple_of(which * half + (n - tiles * (1 - theirs)) * TILE, TILE)
                slot = lax.rem(n, 2)
                return pltpu.make_async_copy(k.streamed.at[:, pl.ds(column, TILE)], k.stream.at[slot], k.stream_sem.at[slot])

            def to_partner(n):
                return send(k.sent.at[n], k.came.at[n], k.pair_send.at[n], k.pair_recv.at[n], {"c": 1 - c})

            @when(0)
            def _():
                fetch(i).start()

        for step in sorted(events):

            @pl.when(i == step)
            def _(step=step):
                for f in events[step]:
                    f()

        if product:

            @pl.when(jnp.logical_and(i >= 1, i <= tiles))
            def _():
                to_partner(i - 1).start()

            @pl.when(i < 2 * tiles)
            def _():
                fetch(i).wait()

                @pl.when(i + 1 < 2 * tiles)
                def _():
                    fetch(i + 1).start()

                block = k.stream[lax.rem(i, 2)]
                if kind == "columns":
                    value = jnp.dot(k.resident[...], block, preferred_element_type=F32)
                else:
                    value = lax.dot_general(block, k.resident[...], (((0,), (0,)), ((), ())), preferred_element_type=F32)

                @pl.when(i < tiles)
                def _():
                    k.sent[i] = value.astype(BF16)

                @pl.when(i >= tiles)
                def _():
                    to_partner(i - tiles).wait()
                    both = value + k.came[i - tiles].astype(F32)
                    k.wide[...] = both
                    k.narrow[...] = both.astype(BF16)

    call = pl.pallas_call(
        kernel,
        grid=(steps,),
        out_shape=out_shapes,
        in_specs=in_specs,
        out_specs=out_specs,
        scratch_shapes=scratch,
        compiler_params=pltpu.CompilerParams(
            collective_id=number, has_side_effects=True, dimension_semantics=("arbitrary",), vmem_limit_bytes=62 * 1024 * 1024
        ),
        cost_estimate=pl.CostEstimate(flops=max(flops, 10**9), bytes_accessed=max(moved, 10**6), transcendentals=0),
        name=f"gradient{number}",
    )
    return dict(zip(names_out, call(*operands), strict=True))


def plane_sum(number, value, chips):
    count = 2 * chips

    def kernel(value_ref, total_ref, got, send_sem, recv_sem):
        q, c = lax.axis_index("q"), lax.axis_index("c")
        me = 2 * q + c
        barrier = pltpu.get_barrier_semaphore()
        peers = [lax.rem(me + n, count) for n in range(1, count)]
        for peer in peers:
            pl.semaphore_signal(barrier, inc=1, device_id={"q": peer // 2, "c": lax.rem(peer, 2)}, device_id_type=MESH)
        pl.semaphore_wait(barrier, count - 1)
        copies = [
            pltpu.make_async_remote_copy(
                src_ref=value_ref,
                dst_ref=got.at[n],
                send_sem=send_sem.at[n],
                recv_sem=recv_sem.at[n],
                device_id={"q": peer // 2, "c": lax.rem(peer, 2)},
                device_id_type=MESH,
            )
            for n, peer in enumerate(peers)
        ]
        for copy in copies:
            copy.start()
        for copy in copies:
            copy.wait()
        total = value_ref[...]
        for n in range(count - 1):
            total = total + got[n]
        total_ref[...] = total

    return pl.pallas_call(
        kernel,
        out_shape=jax.ShapeDtypeStruct((8, 128), F32),
        in_specs=[pl.BlockSpec(memory_space=pltpu.VMEM)],
        out_specs=pl.BlockSpec(memory_space=pltpu.VMEM),
        scratch_shapes=[pltpu.VMEM((count - 1, 8, 128), F32), pltpu.SemaphoreType.DMA((count - 1,)), pltpu.SemaphoreType.DMA((count - 1,))],
        compiler_params=pltpu.CompilerParams(collective_id=number, has_side_effects=True),
        name="plane_sum",
    )(jnp.full((8, 128), value, F32))[0, 0]


def solution(mesh):
    reps, groups, shards = (mesh.shape[a] for a in ("rep", "r", "s"))
    chips = shards // 2
    fine = Mesh(mesh.devices.reshape(reps, groups, chips, 2), ("rep", "r", "q", "c"))
    from_half = [(2 * (s % chips) + s // chips, s) for s in range(shards)]

    def step(x, dy, *arrays):
        weights, m, v = (arrays[i : i + 3] for i in (0, 3, 6))
        layers = weights[0].shape[0]
        first = lax.axis_index("c") == 0

        def own(name, total):
            if name == 2:
                return lax.ppermute(total, ("q", "c"), from_half)
            low, high = jnp.split(total, 2, axis=0)
            keep, send = jnp.where(first, low, high), jnp.where(first, high, low)
            came = lax.ppermute(send, "c", SWAP)
            return jnp.concatenate([jnp.where(first, keep, came), jnp.where(first, came, keep)], 1)

        full = [[lax.all_gather(w[number], ("q", "c"), axis=0, tiled=True) for w in weights] for number in range(layers)]
        h, kept = x[0], []
        for number in range(layers):
            w = full[number]
            a, back = jax.vjp(normed, h)
            gate = jnp.dot(a, w[0], preferred_element_type=F32)
            up = jnp.dot(a, w[1], preferred_element_type=F32)
            act = (jax.nn.silu(gate) * up).astype(BF16)
            kept.append((a, back, gate, up, act))
            if number < layers - 1:
                h = h + matmul(act, w[2])

        queue, totals = [], [[None] * layers for _ in range(3)]
        state = {"number": 0, "scatter": None, "across": None}

        def run(product=None, name=None, number=None):
            s, t = state["scatter"], state["across"]
            given = gradient_call(state["number"], product, s and s[1], None if t is None else t[1])
            state["number"] += 1
            state["scatter"] = state["across"] = None
            if t is not None:
                totals[t[0][0]][t[0][1]] = given["total"]
            if s is not None:
                state["across"] = (s[0], given["block"])
            if product is not None:
                shape = (SIDE, SIDE, given["wide"].shape[0] // chips, given["wide"].shape[1])
                state["scatter"] = ((name, number), (given["wide"].reshape(shape), given["narrow"].reshape(shape)))

        by_h = dy[0]
        for number in reversed(range(layers)):
            w = full[number]
            a, back, gate, up, act = kept[number]
            across_tokens = a.T
            run(("rows", by_h, act), 2, number)
            by_act = lax.dot_general(by_h, w[2], (((1,), (1,)), ((), ())), preferred_element_type=F32).astype(BF16).astype(F32)
            on = jax.nn.sigmoid(gate)
            by_up = (by_act * (gate * on)).astype(BF16)
            by_gate = (by_act * up * (on * (1.0 + gate * (1.0 - on)))).astype(BF16)
            run(("columns", across_tokens, by_gate), 0, number)
            run(("columns", across_tokens, by_up), 1, number)
            if number > 0:
                by_a = [
                    lax.dot_general(by, w[i], (((1,), (1,)), ((), ())), preferred_element_type=F32).astype(BF16) for i, by in ((0, by_gate), (1, by_up))
                ]
                by_h = by_h + back(by_a[0] + by_a[1])[0]
        run()
        run()

        squares = sum(jnp.sum(t.astype(F32) ** 2) for one in totals for t in one)
        squares = plane_sum(state["number"], squares, chips)
        gradients = [jnp.stack([own(name, t) for t in one]).astype(F32) for name, one in enumerate(totals)]
        count = shards * sum(g.size for g in gradients)
        factor = jnp.minimum(1.0, 0.5 * lax.rsqrt(squares / count + 1e-30))
        new = [adamw(w.astype(F32), m, v, g * factor) for w, m, v, g in zip(weights, m, v, gradients, strict=True)]
        return tuple(one[which] for which in range(3) for one in new)

    states, cut = P(("rep", "r", "q", "c"), None, None), P(None, ("q", "c"), None)
    return jax.shard_map(
        step,
        mesh=fine,
        in_specs=(states, states) + (cut,) * 9,
        out_specs=(P("rep", ("q", "c"), None),) * 9,
        check_vma=False,
    )
```

time: 1230 us -> 880 us (0.72)
  waiting for transfers between devices: 633 us -> 171 us
  Pallas kernels: 0 us -> 307 us
  matrix products: 451 us -> 281 us
  blocking collectives: 63.4 us -> 0 us
  starting transfers between devices: 0.53 us -> 16.1 us
  other arithmetic: 30.9 us -> 45.5 us
    reduce_scatter x6 -> x0, waiting for transfers between devices: 401 us -> none  [summed(): lax.psum_scatter(term, 's', scatter_dimension=0, tiled=True)]
    pallas_call x0 -> x9, Pallas kernels: none -> 307 us  [the longest x8 295 us: gradient_call(): return dict(zip(names_out, call(*operands), strict=True))]
    dot_general x15 -> x9, matrix products: 451 us -> 281 us  [the longest x2 82 us: step(): up = jnp.dot(a, w[1], preferred_element_type=F32)]
    psum x1 -> x0, blocking collectives: 63.4 us -> none  [step(): squares = lax.psum(sum((jnp.sum(g * g) for g in gradients)), 's')]
    psum x1 -> x0, waiting for transfers between devices: 56.3 us -> none  [summed(): lax.psum(lax.psum_scatter(term, 's', scatter_dimension=0, tiled=True), 'r')]
    ppermute x0 -> x6, starting transfers between devices: none -> 15.9 us  [the longest x4 9.87 us: own(): came = lax.ppermute(send, 'c', SWAP)]
    add x0 -> x1, other arithmetic: none -> 12.3 us  [step(): by_h = by_h + back(by_a[0] + by_a[1])[0]]
    add_any x1 -> x0, other arithmetic: 12.3 us -> none  [normed(): wide = h.astype(jnp.float32)]
  transfers between devices with their start and end apart: 13 -> 12, of which waited for: 12 -> 6; matrix products, arithmetic and copies ran while one was open for 29% -> 21% of each run, Pallas kernels for 0% -> 1%
where the time goes in v2:
time: 880 us; the launch traced here: 873 us
  Pallas kernels  307 us (35%)
  matrix products  281 us (32%)
  waiting for transfers between devices  171 us (19%)
  other arithmetic  45.5 us (5%)
  local copies, waits for them, and re-layouts  32.4 us (4%)
  between operations  19.5 us (2%)
  starting transfers between devices  16.1 us (2%)
    pallas_call x8, Pallas kernels, gradient_call(): return dict(zip(names_out, call(*operands), strict=True))  295 us
    all_gather x6, waiting for transfers between devices, step(): lax.all_gather(w[number], ('q', 'c'), axis=0, tiled=True)  169 us
    dot_general x2, matrix products, step(): up = jnp.dot(a, w[1], preferred_element_type=F32)  82 us
    dot_general x2, matrix products, step(): lax.dot_general(by_h, w[2], (((1,), (1,)), ((), ())), preferred_element_t...  70 us
    dot_general x2, matrix products, step(): gate = jnp.dot(a, w[0], preferred_element_type=F32)  53.9 us
    dot_general x2, matrix products, step(): lax.dot_general(by, w[i], (((1,), (1,)), ((), ())), preferred_element_typ...  48.5 us
    dot_general x1, matrix products, matmul(): return jnp.dot(a, w, preferred_element_type=F32).astype(BF16)  26.8 us
  transfers between devices with their start and end apart: 12, of which 6 were waited for; matrix products, arithmetic and copies ran while one was open for 21% of the time, Pallas kernels for 1%

profile of v2, /device:TPU:1, one launch (start us, length us, event | category | flops | bytes accessed | tf_op | source)
XLA Modules:
  0.0 872.6 jit_solution(11526860376074092682)
XLA Ops:
  38.5 30.4 %all-gather.15.cloned.1.call-done = bf16[1,1280,3584]{2,1,0:T(8,128)(2,1)} async-done(((bf16[1,40,3584]{2,1,0:T(8,128)(2,1)}), bf16[1,1280,3584]{2,1,0:T(8,128)(2,1)}) %all-gather.15.cloned.1.call-update) | async-done | bytes 9175056 | tf_op jit(solution)/shard_map/all_gather | solution.py:418
  68.9 27.0 %fusion.28 = f32[2048,3584]{1,0:T(8,128)} fusion(bf16[1,1280,3584]{2,1,0:T(8,128)(2,1)} %all-gather.15.cloned.1.call-done, bf16[1,2048,1280]{1,2,0:T(8,128)(2,1)} %copy.20, f32[2048]{0:T(1024)S(1)} %add_rsqrt_fusion), kind=kOutput, calls=%fused_computation.45 | convolution fusion | flops 18798346240 | bytes 43786240 | tf_op jit(solution)/shard_map/dot_general | solution.py:423
  95.9 29.8 %all-gather.17.cloned.1.call-done = bf16[1,1280,3584]{2,1,0:T(8,128)(2,1)} async-done(((bf16[1,40,3584]{2,1,0:T(8,128)(2,1)}), bf16[1,1280,3584]{2,1,0:T(8,128)(2,1)}) %all-gather.17.cloned.1.call-update) | async-done | bytes 9175056 | tf_op jit(solution)/shard_map/all_gather | solution.py:418
  125.7 36.9 %multiply_convert_fusion.1 = (bf16[2048,3584]{1,0:T(8,128)(2,1)}, f32[2048,3584]{1,0:T(8,128)}) fusion(f32[2048,3584]{1,0:T(8,128)} %fusion.28, bf16[1,1280,3584]{2,1,0:T(8,128)(2,1)} %all-gather.17.cloned.1.call-done, bf16[1,2048,1280]{1,2,0:T(8,128)(2,1)} %copy.20, f32[2048]{0:T(1024)S(1)} %add_rsqrt_fusion), kind=kOutput, calls=%fused_computation.13 | convolution fusion | flops 18842386432 | bytes 87826432 | tf_op jit(solution)/shard_map/dot_general | solution.py:424
  162.5 19.9 %all-gather.19.cloned.1.call-done = bf16[1,3584,1280]{2,1,0:T(8,128)(2,1)} async-done(((bf16[1,112,1280]{2,1,0:T(8,128)(2,1)}), bf16[1,3584,1280]{2,1,0:T(8,128)(2,1)}) %all-gather.19.cloned.1.call-update) | async-done | bytes 9175056 | tf_op jit(solution)/shard_map/all_gather | solution.py:418
  182.5 26.8 %fusion.12 = (f32[2048]{0:T(1024)S(1)}, bf16[2048,1280]{0,1:T(8,128)(2,1)}) fusion(bf16[2048,3584]{1,0:T(8,128)(2,1)} %get-tuple-element.85.refs_1_, bf16[1,3584,1280]{2,1,0:T(8,128)(2,1)} %all-gather.19.cloned.1.call-done, bf16[1,2048,1280]{1,2,0:T(8,128)(2,1)} %copy.20), kind=kOutput, calls=%fused_computation.29 | convolution fusion | flops 18803587072 | bytes 34349056 | tf_op jit(solution)/shard_map/dot_general | solution.py:20
  209.9 29.2 %all-gather.13.cloned.1.call-done = bf16[1,3584,1280]{2,1,0:T(8,128)(2,1)} async-done(((bf16[1,112,1280]{2,1,0:T(8,128)(2,1)}), bf16[1,3584,1280]{2,1,0:T(8,128)(2,1)}) %all-gather.13.cloned.1.call-update) | async-done | bytes 9175056 | tf_op jit(solution)/shard_map/all_gather | solution.py:418
  239.1 26.2 %convolution_convert_fusion.1 = bf16[2048,3584]{1,0:T(8,128)(2,1)} fusion(bf16[1,3584,1280]{2,1,0:T(8,128)(2,1)} %all-gather.13.cloned.1.call-done, bf16[1,2048,1280]{2,1,0:T(8,128)(2,1)} %param.12), kind=kOutput, calls=%fused_computation.21 | convolution fusion | flops 18797821952 | bytes 29097984 | tf_op jit(solution)/shard_map/dot_general | solution.py:452
  265.3 30.4 %all-gather.23.cloned.1.call-done = bf16[1,1280,3584]{2,1,0:T(8,128)(2,1)} async-done(((bf16[1,40,3584]{2,1,0:T(8,128)(2,1)}), bf16[1,1280,3584]{2,1,0:T(8,128)(2,1)}) %all-gather.23.cloned.1.call-update) | async-done | bytes 9175056 | tf_op jit(solution)/shard_map/all_gather | solution.py:418
  295.7 27.0 %fusion.17 = f32[2048,3584]{1,0:T(8,128)} fusion(bf16[1,1280,3584]{2,1,0:T(8,128)(2,1)} %all-gather.23.cloned.1.call-done, bf16[2048,1280]{0,1:T(8,128)(2,1)} %get-tuple-element.88, f32[2048]{0:T(1024)S(1)} %fusion.65), kind=kOutput, calls=%fused_computation.34 | convolution fusion | flops 18798346240 | bytes 43786240 | tf_op jit(solution)/shard_map/dot_general | solution.py:423
  322.7 29.7 %all-gather.21.cloned.1.call-done = bf16[1,1280,3584]{2,1,0:T(8,128)(2,1)} async-done(((bf16[1,40,3584]{2,1,0:T(8,128)(2,1)}), bf16[1,1280,3584]{2,1,0:T(8,128)(2,1)}) %all-gather.21.cloned.1.call-update) | async-done | bytes 9175056 | tf_op jit(solution)/shard_map/all_gather | solution.py:418
  352.3 45.1 %multiply_convert_fusion = (bf16[2048,3584]{1,0:T(8,128)(2,1)}, bf16[2048,3584]{1,0:T(8,128)(2,1)}, bf16[2048,3584]{1,0:T(8,128)(2,1)}) fusion(f32[2048,3584]{1,0:T(8,128)} %fusion.17, bf16[2048,3584]{1,0:T(8,128)(2,1)} %convolution_convert_fusion.1, bf16[1,1280,3584]{2,1,0:T(8,128)(2,1)} %all-gather.21.cloned.1.call-done, ...), kind=kOutput, calls=%fused_computation.10 | convolution fusion | flops 18915786752 | bytes 102506496 | tf_op jit(solution)/shard_map/dot_general | solution.py:424
  397.5 25.8 %fusion.34 = bf16[2048,1280]{0,1:T(8,128)(2,1)} fusion(bf16[2048,3584]{1,0:T(8,128)(2,1)} %get-tuple-element.66.refs_1_, bf16[1,1280,3584]{2,1,0:T(8,128)(2,1)} %all-gather.21.cloned.1.call-done), kind=kOutput, calls=%fused_computation.49 | convolution fusion | flops 18793103360 | bytes 29097984 | tf_op jit(solution)/shard_map/dot_general | solution.py:460
  423.3 22.7 %fusion.40 = bf16[2048,1280]{0,1:T(8,128)(2,1)S(1)} fusion(bf16[2048,1280]{0,1:T(8,128)(2,1)} %fusion.34, bf16[2048,3584]{1,0:T(8,128)(2,1)} %get-tuple-element.65.refs_1_, bf16[1,1280,3584]{2,1,0:T(8,128)(2,1)S(1)} %copy-done.17), kind=kOutput, calls=%fused_computation.51 | convolution fusion | flops 18795724800 | bytes 34340864 | tf_op jit(solution)/shard_map/dot_general | solution.py:460
  451.2 12.3 %fusion.46 = bf16[2048,1280]{0,1:T(8,128)(2,1)} fusion(bf16[2048,1280]{0,1:T(8,128)(2,1)} %get-tuple-element.88, bf16[2048,1280]{0,1:T(8,128)(2,1)} %copy-done.1, bf16[1,2048,1280]{1,2,0:T(8,128)(2,1)} %copy.21, f32[2048]{0:T(1024)S(1)} %multiply_multiply_fusion.3, f32[2048]{0:T(1024)S(1)} %fusion.65), kind=kLoop, calls=%fused_computation.53 | loop fusion | flops 18350080 | bytes 20987904 | tf_op jit(solution)/shard_map/add | solution.py:462
  471.5 30.3 %gradient0.1 = (f32[1792,1280]{1,0:T(8,128)}, bf16[1792,1280]{1,0:T(8,128)(2,1)}) custom-call(bf16[2048,1280]{1,0:T(8,128)(2,1)} %bitcast.93, bf16[2048,3584]{1,0:T(8,128)(2,1)} %get-tuple-element.64.refs_1_), custom_call_target="tpu_custom_call" | custom-call | flops 18790481920 | bytes 33685504 | tf_op jit(solution)/shard_map/gradient0/pallas_call | solution.py:354
  501.8 43.1 %gradient1.1 = (f32[1280,1792]{1,0:T(8,128)}, bf16[1280,1792]{1,0:T(8,128)(2,1)}, bf16[112,1280]{1,0:T(8,128)(2,1)}) custom-call(bf16[1280,2048]{1,0:T(8,128)(2,1)} %get-tuple-element.69.refs_0_, bf16[2048,3584]{1,0:T(8,128)(2,1)} %get-tuple-element.65.refs_1_, f32[4,4,112,1280]{3,2,1,0:T(8,128)} %bitcast.99, bf16[4,4,112,1280]{3,2,1,0:T(8,128)(2,1)} %bitcast.104), custom_call_target="tpu_custom_call" | custom-call | flops 18790481920 | bytes 33685504 | tf_op jit(solution)/shard_map/gradient1/pallas_call | solution.py:354
  544.9 44.5 %gradient2.1 = (f32[1280,1792]{1,0:T(8,128)}, bf16[1280,1792]{1,0:T(8,128)(2,1)}, bf16[80,1792]{1,0:T(8,128)(2,1)}, bf16[112,1280]{1,0:T(8,128)(2,1)}) custom-call(bf16[1280,2048]{1,0:T(8,128)(2,1)} %get-tuple-element.69.refs_0_, bf16[2048,3584]{1,0:T(8,128)(2,1)} %get-tuple-element.66.refs_1_, f32[4,4,80,1792]{3,2,1,0:T(8,128)} %bitcast.98, ...), custom_call_target="tpu_custom_call" | custom-call | flops 18790481920 | bytes 33685504 | tf_op jit(solution)/shard_map/gradient2/pallas_call | solution.py:354
  589.5 48.4 %gradient3.1 = (f32[1792,1280]{1,0:T(8,128)}, bf16[1792,1280]{1,0:T(8,128)(2,1)}, bf16[80,1792]{1,0:T(8,128)(2,1)}, bf16[80,1792]{1,0:T(8,128)(2,1)}) custom-call(bf16[2048,1280]{1,0:T(8,128)(2,1)} %copy.23.refs_0_, bf16[2048,3584]{1,0:T(8,128)(2,1)} %get-tuple-element.85.refs_1_, f32[4,4,80,1792]{3,2,1,0:T(8,128)} %bitcast.96, ...), custom_call_target="tpu_custom_call" | custom-call | flops 18790481920 | bytes 33685504 | tf_op jit(solution)/shard_map/gradient3/pallas_call | solution.py:354
  637.8 43.8 %fusion.5 = (bf16[2048,3584]{1,0:T(8,128)(2,1)}, bf16[2048,3584]{1,0:T(8,128)(2,1)}) fusion(f32[2048,3584]{1,0:T(8,128)} %get-tuple-element.86, f32[2048,3584]{1,0:T(8,128)} %fusion.28, bf16[2048,1280]{0,1:T(8,128)(2,1)} %fusion.46, bf16[1,3584,1280]{2,1,0:T(8,128)(2,1)} %all-gather.19.cloned.1.call-done), kind=kOutput, calls=%fused_computation.9 | convolution fusion | flops 18900582400 | bytes 102498304 | tf_op jit(solution)/shard_map/dot_general | solution.py:452
  681.6 42.7 %gradient4.1 = (f32[1280,1792]{1,0:T(8,128)}, bf16[1280,1792]{1,0:T(8,128)(2,1)}, bf16[112,1280]{1,0:T(8,128)(2,1)}, bf16[80,1792]{1,0:T(8,128)(2,1)}) custom-call(bf16[1280,2048]{1,0:T(8,128)(2,1)} %fusion.52.refs_0_, bf16[2048,3584]{1,0:T(8,128)(2,1)} %get-tuple-element.67.refs_1_, f32[4,4,112,1280]{3,2,1,0:T(8,128)} %bitcast.95, ...), custom_call_target="tpu_custom_call" | custom-call | flops 18790481920 | bytes 33685504 | tf_op jit(solution)/shard_map/gradient4/pallas_call | solution.py:354
  724.3 44.5 %gradient5.1 = (f32[1280,1792]{1,0:T(8,128)}, bf16[1280,1792]{1,0:T(8,128)(2,1)}, bf16[80,1792]{1,0:T(8,128)(2,1)}, bf16[112,1280]{1,0:T(8,128)(2,1)}) custom-call(bf16[1280,2048]{1,0:T(8,128)(2,1)} %fusion.52.refs_0_, bf16[2048,3584]{1,0:T(8,128)(2,1)} %get-tuple-element.68.refs_1_, f32[4,4,80,1792]{3,2,1,0:T(8,128)} %bitcast.97, ...), custom_call_target="tpu_custom_call" | custom-call | flops 18790481920 | bytes 33685504 | tf_op jit(solution)/shard_map/gradient5/pallas_call | solution.py:354
  768.9 31.5 %gradient6.1 = (bf16[80,1792]{1,0:T(8,128)(2,1)}, bf16[80,1792]{1,0:T(8,128)(2,1)}) custom-call(f32[4,4,80,1792]{3,2,1,0:T(8,128)} %bitcast.92, bf16[4,4,80,1792]{3,2,1,0:T(8,128)(2,1)} %bitcast.94, bf16[80,1792]{1,0:T(8,128)(2,1)} %get-tuple-element.48.refs_2_), custom_call_target="tpu_custom_call" | custom-call | flops 1000000000 | bytes 1000000 | tf_op jit(solution)/shard_map/gradient6/pallas_call | solution.py:354
  842.5 12.2 %plane_sum.1 = f32[8,128]{1,0:T(8,128)} custom-call(f32[8,128]{1,0:T(8,128)} %broadcast_in_dim.2.value_ref), custom_call_target="tpu_custom_call" | custom-call | tf_op jit(solution)/shard_map/plane_sum/pallas_call | solution.py:388
  (100 shorter events, 92.8 us)
Async XLA Ops:
  7.2 61.7 %all-gather.15.cloned.1.call-start = ((), (), s32[]{:S(2)}) async-start(), calls=%async_computation.1 | async-start | bytes 9461760 | tf_op jit(solution)/shard_map/all_gather | solution.py:418
  9.1 116.5 %all-gather.17.cloned.1.call-start = ((), (), s32[]{:S(2)}) async-start(), calls=%async_computation.2 | async-start | bytes 9461760 | tf_op jit(solution)/shard_map/all_gather | solution.py:418
  11.1 171.4 %all-gather.19.cloned.1.call-start = ((), (), s32[]{:S(2)}) async-start(), calls=%async_computation.3 | async-start | bytes 9461760 | tf_op jit(solution)/shard_map/all_gather | solution.py:418
  13.1 226.0 %all-gather.13.cloned.1.call-start = ((), (), s32[]{:S(2)}) async-start(), calls=%async_computation | async-start | bytes 9461760 | tf_op jit(solution)/shard_map/all_gather | solution.py:418
  13.6 282.1 %all-gather.23.cloned.1.call-start = ((), (), s32[]{:S(2)}) async-start(), calls=%async_computation.5 | async-start | bytes 9461760 | tf_op jit(solution)/shard_map/all_gather | solution.py:418
  14.2 338.1 %all-gather.21.cloned.1.call-start = ((), (), s32[]{:S(2)}) async-start(), calls=%async_computation.4 | async-start | bytes 9461760 | tf_op jit(solution)/shard_map/all_gather | solution.py:418
  397.5 25.8 %copy-start.17 = (bf16[1,1280,3584]{2,1,0:T(8,128)(2,1)S(1)}, bf16[1,1280,3584]{2,1,0:T(8,128)(2,1)}, u32[]{:S(2)}) copy-start(bf16[1,1280,3584]{2,1,0:T(8,128)(2,1)} %all-gather.23.cloned.1.call-done) | copy-start | bytes 27525124
  397.5 48.5 %slice-start = ((s8[5242880]{0:T(1024)(128)(4,1)}), s8[4194304]{0:T(1024)(128)(4,1)S(1)}, s32[]{:S(2)}) async-start(s8[5242880]{0:T(1024)(128)(4,1)} %bitcast.90), calls=%async_computation.6 | async-start | bytes 8388608
  423.3 22.7 %slice-start.1 = ((s8[5242880]{0:T(1024)(128)(4,1)}), s8[1048576]{0:T(1024)(128)(4,1)S(1)}, s32[]{:S(2)}) async-start(s8[5242880]{0:T(1024)(128)(4,1)} %bitcast.90), calls=%async_computation.7 | async-start | bytes 2097152
  446.0 5.2 copy-start.1
  446.0 5.2 copy-start.16
  768.8 33.3 %copy-start.3 = (bf16[80,1792]{1,0:T(8,128)(2,1)S(1)}, bf16[80,1792]{1,0:T(8,128)(2,1)}, u32[]{:S(2)}) copy-start(bf16[80,1792]{1,0:T(8,128)(2,1)} %get-tuple-element.50) | copy-start | bytes 860164
  768.8 36.3 %copy-start.2 = (bf16[80,1792]{1,0:T(8,128)(2,1)S(1)}, bf16[80,1792]{1,0:T(8,128)(2,1)}, u32[]{:S(2)}) copy-start(bf16[80,1792]{1,0:T(8,128)(2,1)} %get-tuple-element.52) | copy-start | bytes 860164
  800.3 58.5 %copy-start.5 = (bf16[80,1792]{1,0:T(8,128)(2,1)S(1)}, bf16[80,1792]{1,0:T(8,128)(2,1)}, u32[]{:S(2)}) copy-start(bf16[80,1792]{1,0:T(8,128)(2,1)} %get-tuple-element.49) | copy-start | bytes 860164
  805.9 53.1 %copy-start.6 = (bf16[2,40,3584]{2,1,0:T(8,128)(2,1)S(1)}, bf16[2,40,3584]{2,1,0:T(8,128)(2,1)}, u32[]{:S(2)}) copy-start(bf16[2,40,3584]{2,1,0:T(8,128)(2,1)} %param.13) | copy-start | bytes 1720324
  805.9 53.1 %copy-start.7 = (bf16[2,40,3584]{2,1,0:T(8,128)(2,1)S(1)}, bf16[2,40,3584]{2,1,0:T(8,128)(2,1)}, u32[]{:S(2)}) copy-start(bf16[2,40,3584]{2,1,0:T(8,128)(2,1)} %param.14) | copy-start | bytes 1720324
  816.2 42.7 %copy-start.4 = (bf16[80,1792]{1,0:T(8,128)(2,1)S(1)}, bf16[80,1792]{1,0:T(8,128)(2,1)}, u32[]{:S(2)}) copy-start(bf16[80,1792]{1,0:T(8,128)(2,1)} %gradient7.1) | copy-start | bytes 860164
  816.2 42.8 %copy-start.9 = (f32[2,40,3584]{2,1,0:T(8,128)S(1)}, f32[2,40,3584]{2,1,0:T(8,128)}, u32[]{:S(2)}) copy-start(f32[2,40,3584]{2,1,0:T(8,128)} %param.19) | copy-start | bytes 3440644
  819.7 37.7 %collective-permute-start.1 = (bf16[40,1792]{1,0:T(8,128)(2,1)}, bf16[40,1792]{1,0:T(8,128)(2,1)}, u32[]{:S(2)}, u32[]{:S(2)}) collective-permute-start(bf16[40,1792]{1,0:T(8,128)(2,1)} %broadcast_select_fusion.10), channel_id=1, source_target_pairs={{0,1},{1,0},{2,3},{3,2},{4,5},{5,4},{6,7},{7,6},{8,9},{9,8},{10,11... | collective-permute-start | bytes 430088 | tf_op jit(solution)/shard_map/ppermute | solution.py:415
  830.3 32.0 %collective-permute-start.4 = (bf16[112,1280]{1,0:T(8,128)(2,1)}, bf16[112,1280]{1,0:T(8,128)(2,1)}, u32[]{:S(2)}, u32[]{:S(2)}) collective-permute-start(bf16[112,1280]{1,0:T(8,128)(2,1)} %get-tuple-element.53), channel_id=1, source_target_pairs={{0,0},{2,1},{4,2},{6,3},{8,4},{10,5},{12,6},{14,7},{16,8},{18,9},{... | collective-permute-start | bytes 860168 | tf_op jit(solution)/shard_map/ppermute | solution.py:412
  833.3 29.1 %collective-permute-start.5 = (bf16[112,1280]{1,0:T(8,128)(2,1)}, bf16[112,1280]{1,0:T(8,128)(2,1)}, u32[]{:S(2)}, u32[]{:S(2)}) collective-permute-start(bf16[112,1280]{1,0:T(8,128)(2,1)} %get-tuple-element.54), channel_id=1, source_target_pairs={{0,0},{2,1},{4,2},{6,3},{8,4},{10,5},{12,6},{14,7},{16,8},{18,9},{... | collective-permute-start | bytes 860168 | tf_op jit(solution)/shard_map/ppermute | solution.py:412
  856.8 2.0 collective-permute-start
  857.3 1.6 collective-permute-start.3
  857.4 1.5 collective-permute-start.2
  (8 other events, 27.4 us)
Sparse Core Ops, SparseCore 0:
  10.8 58.0 all-gather.14
  71.7 53.9 all-gather.16
  128.5 53.9 all-gather.18
  185.1 53.8 all-gather.12
  241.8 53.9 all-gather.22
  298.4 53.9 all-gather.20

commit v3 on v2

--- a/solution.py
+++ b/solution.py
@@ -49,7 +49,7 @@
     pass
 
 
-def gradient_call(number, product=None, scatter=None, across=None):
+def gradient_call(number, product=None, scatter=None, finish=None, across=None):
     operands, in_specs, out_shapes, out_specs, scratch = [], [], [], [], []
     names_in, names_out, names_scratch = [], [], []
     anywhere, vmem = pl.BlockSpec(memory_space=pl.ANY), pl.BlockSpec(memory_space=pltpu.VMEM)
@@ -94,22 +94,30 @@
         wide, narrow = scatter
         rows, columns = wide.shape[2:]
         part = columns // 2
-        cut = upper(rows)
         take("wide_in", wide, anywhere)
         take("narrow_in", narrow, anywhere)
-        give("block", (rows, columns), BF16, vmem)
+        give("kept", (2, SIDE, rows, part), F32, vmem)
+        give("third", (2, rows, part), BF16, vmem)
         hold("held", pltpu.VMEM((2, 3, SIDE, rows, part), F32))
         hold("held_sem", dma((2, 3)))
         hold("got1", pltpu.VMEM((2, 2, 2, rows, part), BF16))
         hold("put2", pltpu.VMEM((2, 2, SIDE, rows, part), BF16))
         hold("got2", pltpu.VMEM((2, 2, SIDE, rows, part), BF16))
-        hold("put3", pltpu.VMEM((2, rows, part), BF16))
-        hold("got3", pltpu.VMEM((2, rows, part), BF16))
-        hold("put4", pltpu.VMEM((2, 2, rows, part), BF16))
-        hold("got4", pltpu.VMEM((2, 2, rows, part), BF16))
-        hold("ring_send", dma((4, 2, 2)))
-        hold("ring_recv", dma((4, 2, 2)))
-        steps = max(steps, 17)
+        hold("ring_send", dma((2, 2, 2)))
+        hold("ring_recv", dma((2, 2, 2)))
+        steps = max(steps, 13)
+    if finish:
+        last_rows, last_part = finish[1].shape[1:]
+        cut = upper(last_rows)
+        take("kept_in", finish[0], vmem)
+        take("third_in", finish[1], vmem)
+        give("block", (last_rows, 2 * last_part), BF16, vmem)
+        hold("got3", pltpu.VMEM((2, last_rows, last_part), BF16))
+        hold("put4", pltpu.VMEM((2, 2, last_rows, last_part), BF16))
+        hold("got4", pltpu.VMEM((2, 2, last_rows, last_part), BF16))
+        hold("last_send", dma((2, 2, 2)))
+        hold("last_recv", dma((2, 2, 2)))
+        steps = max(steps, 10)
     if across is not None:
         wide_rows, wide_columns = across.shape
         take("partial", across, vmem)
@@ -135,7 +143,7 @@
         peers = []
         if product:
             peers.append({"c": 1 - c})
-        if scatter:
+        if scatter or finish:
             peers += [beside(axis, by) for axis in (0, 1) for by in (1, -1)]
         if across is not None:
             peers += [{"r": near(x)}, {"r": wrap(x)}]
@@ -159,11 +167,11 @@
                 pl.semaphore_signal(barrier, inc=1, device_id=peer, device_id_type=MESH)
             pl.semaphore_wait(barrier, len(peers))
 
+        def places(p, by):
+            return lax.rem(at[p] + by + SIDE, SIDE)
+
         if scatter:
             spans = (pl.ds(0, part), pl.ds(part, part))
-
-            def places(p, by):
-                return lax.rem(at[p] + by + SIDE, SIDE)
 
             def of(ref, p, by, some):
                 return ref.at[places(p, by), some, :, spans[p]] if p == 0 else ref.at[some, places(p, by), :, spans[p]]
@@ -181,13 +189,8 @@
                     for n, by in enumerate((1, -1)):
                         if stage == 0:
                             src, dst, axis = of(k.narrow_in, p, 2, pl.ds(2 * n, 2)), k.got1.at[p, n], p
-                        elif stage == 1:
+                        else:
                             src, dst, axis = k.put2.at[p, n], k.got2.at[p, n], p
-                        elif stage == 2:
-                            some = pl.ds(0, cut) if n == 0 else pl.ds(cut, rows - cut)
-                            src, dst, axis = k.put3.at[p, some], k.got3.at[p, some], 1 - p
-                        else:
-                            src, dst, axis = k.put4.at[p, n], k.got4.at[p, n], 1 - p
                         copies.append(send(src, dst, k.ring_send.at[stage, p, n], k.ring_recv.at[stage, p, n], beside(axis, by)))
                 return copies
 
@@ -219,37 +222,52 @@
                     copy.wait()
                 for p in (0, 1):
                     for s in range(SIDE):
-                        k.held[p, 0, s] = k.held[p, 0, s] + k.got2[p, 0, s].astype(F32) + k.got2[p, 1, s].astype(F32)
-                    k.put3[p] = k.held[p, 0, places(1 - p, 2)].astype(BF16)
-
-            @when(13)
-            def _():
-                for copy in ring(2):
+                        k.kept[p, s] = k.held[p, 0, s] + k.got2[p, 0, s].astype(F32) + k.got2[p, 1, s].astype(F32)
+                    k.third[p] = k.kept[p, places(1 - p, 2)].astype(BF16)
+
+        if finish:
+
+            def last(stage):
+                copies = []
+                for p in (0, 1):
+                    for n, by in enumerate((1, -1)):
+                        if stage == 0:
+                            some = pl.ds(0, cut) if n == 0 else pl.ds(cut, last_rows - cut)
+                            src, dst = k.third_in.at[p, some], k.got3.at[p, some]
+                        else:
+                            src, dst = k.put4.at[p, n], k.got4.at[p, n]
+                        copies.append(send(src, dst, k.last_send.at[stage, p, n], k.last_recv.at[stage, p, n], beside(1 - p, by)))
+                return copies
+
+            @when(0)
+            def _():
+                for copy in last(0):
                     copy.start()
 
-            @when(14)
-            def _():
-                for copy in ring(2):
+            @when(3)
+            def _():
+                for copy in last(0):
                     copy.wait()
                 for p in (0, 1):
                     ahead, behind = places(1 - p, 1), places(1 - p, -1)
-                    k.put4[p, 0, :cut] = (k.held[p, 0, ahead, :cut] + k.got3[p, :cut].astype(F32)).astype(BF16)
-                    k.put4[p, 0, cut:] = k.held[p, 0, ahead, cut:].astype(BF16)
-                    k.put4[p, 1, :cut] = k.held[p, 0, behind, :cut].astype(BF16)
-                    k.put4[p, 1, cut:] = (k.held[p, 0, behind, cut:] + k.got3[p, cut:].astype(F32)).astype(BF16)
-
-            @when(15)
-            def _():
-                for copy in ring(3):
+                    k.put4[p, 0, :cut] = (k.kept_in[p, ahead, :cut] + k.got3[p, :cut].astype(F32)).astype(BF16)
+                    k.put4[p, 0, cut:] = k.kept_in[p, ahead, cut:].astype(BF16)
+                    k.put4[p, 1, :cut] = k.kept_in[p, behind, :cut].astype(BF16)
+                    k.put4[p, 1, cut:] = (k.kept_in[p, behind, cut:] + k.got3[p, cut:].astype(F32)).astype(BF16)
+
+            @when(4)
+            def _():
+                for copy in last(1):
                     copy.start()
 
-            @when(16)
-            def _():
-                for copy in ring(3):
+            @when(9)
+            def _():
+                for copy in last(1):
                     copy.wait()
                 for p in (0, 1):
-                    mine = k.held[p, 0, places(1 - p, 0)]
-                    k.block[:, p * part : (p + 1) * part] = (mine + k.got4[p, 0].astype(F32) + k.got4[p, 1].astype(F32)).astype(BF16)
+                    mine = k.kept_in[p, places(1 - p, 0)]
+                    both = mine + k.got4[p, 0].astype(F32) + k.got4[p, 1].astype(F32)
+                    k.block[:, p * last_part : (p + 1) * last_part] = both.astype(BF16)
 
         if across is not None:
             sides = (pl.ds(0, wide_columns // 2), pl.ds(wide_columns // 2, wide_columns // 2))
@@ -352,6 +370,110 @@
         name=f"gradient{number}",
     )
     return dict(zip(names_out, call(*operands), strict=True))
+
+
+def gathered_pair(number, one, two):
+    rows, columns = one.shape[1:]
+    halves = (pl.ds(0, columns // 2), pl.ds(columns // 2, columns // 2))
+    every = pl.ds(0, SIDE)
+    dma = pltpu.SemaphoreType.DMA
+
+    def kernel(one_ref, two_ref, one_out, two_out, own_sem, ring_send, ring_recv, pair_send, pair_recv):
+        q, c = lax.axis_index("q"), lax.axis_index("c")
+        at = (q // SIDE, lax.rem(q, SIDE))
+        ins, outs = (one_ref, two_ref), (one_out, two_out)
+
+        def along(axis, by):
+            return lax.rem(at[axis] + by + SIDE, SIDE)
+
+        def beside(axis, by):
+            return {"q": along(0, by) * SIDE + at[1] if axis == 0 else at[0] * SIDE + along(1, by)}
+
+        def line(p, by, some=None):
+            there = along(1 - p, by)
+            some = pl.ds(0, columns) if some is None else some
+            return outs[p].at[every, there, c, :, some] if p == 0 else outs[p].at[there, every, c, :, some]
+
+        def single(p, by, some=None):
+            there = along(p, by)
+            some = pl.ds(0, columns) if some is None else some
+            return outs[p].at[there, at[1], c, :, some] if p == 0 else outs[p].at[at[0], there, c, :, some]
+
+        def send(src, dst, stage, p, n, to):
+            return pltpu.make_async_remote_copy(
+                src_ref=src, dst_ref=dst, send_sem=ring_send.at[stage, p, n], recv_sem=ring_recv.at[stage, p, n], device_id=to, device_id_type=MESH
+            )
+
+        def ring(stage):
+            copies = []
+            for p in (0, 1):
+                for n, by in enumerate((1, -1)):
+                    if stage == 0:
+                        copies.append(send(ins[p].at[0], single(p, 0), stage, p, n, beside(p, by)))
+                    elif stage == 1:
+                        copies.append(send(single(p, -by, halves[n]), single(p, -by, halves[n]), stage, p, n, beside(p, by)))
+                    elif stage == 2:
+                        copies.append(send(line(p, 0), line(p, 0), stage, p, n, beside(1 - p, by)))
+                    else:
+                        copies.append(send(line(p, -by, halves[n]), line(p, -by, halves[n]), stage, p, n, beside(1 - p, by)))
+            return copies
+
+        def to_partner(by, n):
+            return [
+                pltpu.make_async_remote_copy(
+                    src_ref=line(p, by),
+                    dst_ref=line(p, by),
+                    send_sem=pair_send.at[p, n],
+                    recv_sem=pair_recv.at[p, n],
+                    device_id={"c": 1 - c},
+                    device_id_type=MESH,
+                )
+                for p in (0, 1)
+            ]
+
+        def start(copies):
+            for copy in copies:
+                copy.start()
+
+        def wait(copies):
+            for copy in copies:
+                copy.wait()
+
+        barrier = pltpu.get_barrier_semaphore()
+        for peer in [{"c": 1 - c}] + [beside(axis, by) for axis in (0, 1) for by in (1, -1)]:
+            pl.semaphore_signal(barrier, inc=1, device_id=peer, device_id_type=MESH)
+        pl.semaphore_wait(barrier, 5)
+
+        own = [pltpu.make_async_copy(ins[p].at[0], single(p, 0), own_sem.at[p]) for p in (0, 1)]
+        start(ring(0))
+        start(own)
+        wait(ring(0))
+        start(ring(1))
+        wait(own)
+        wait(ring(1))
+        start(ring(2))
+        start(to_partner(0, 0))
+        wait(ring(2))
+        start(ring(3))
+        start(to_partner(1, 1))
+        start(to_partner(-1, 2))
+        wait(ring(3))
+        start(to_partner(2, 3))
+        for n, by in enumerate((0, 1, -1, 2)):
+            wait(to_partner(by, n))
+
+    shape = (SIDE, SIDE, 2, rows, columns)
+    outs = pl.pallas_call(
+        kernel,
+        out_shape=[jax.ShapeDtypeStruct(shape, BF16)] * 2,
+        in_specs=[pl.BlockSpec(memory_space=pltpu.VMEM)] * 2,
+        out_specs=[pl.BlockSpec(memory_space=pl.ANY)] * 2,
+        scratch_shapes=[dma((2,)), dma((4, 2, 2)), dma((4, 2, 2)), dma((2, 4)), dma((2, 4))],
+        compiler_params=pltpu.CompilerParams(collective_id=number, has_side_effects=True),
+        cost_estimate=pl.CostEstimate(flops=2 * 10**10, bytes_accessed=4 * 10**7, transcendentals=0),
+        name="gathered_pair",
+    )(one, two)
+    return [out.reshape(SIDE * SIDE * 2 * rows, columns) for out in outs]
 
 
 def plane_sum(number, value, chips):
@@ -415,7 +537,10 @@
             came = lax.ppermute(send, "c", SWAP)
             return jnp.concatenate([jnp.where(first, keep, came), jnp.where(first, came, keep)], 1)
 
-        full = [[lax.all_gather(w[number], ("q", "c"), axis=0, tiled=True) for w in weights] for number in range(layers)]
+        full = [
+            [None if number == 0 and i < 2 else lax.all_gather(w[number], ("q", "c"), axis=0, tiled=True) for i, w in enumerate(weights)] for number in range(layers)
+        ]
+        full[0][:2] = gathered_pair(12, weights[0], weights[1])
         h, kept = x[0], []
         for number in range(layers):
             w = full[number]
@@ -427,18 +552,18 @@
             if number < layers - 1:
                 h = h + matmul(act, w[2])
 
-        queue, totals = [], [[None] * layers for _ in range(3)]
-        state = {"number": 0, "scatter": None, "across": None}
+        totals = [[None] * layers for _ in range(3)]
+        state = {"number": 0, "scatter": None, "finish": None, "across": None}
 
         def run(product=None, name=None, number=None):
-            s, t = state["scatter"], state["across"]
-            given = gradient_call(state["number"], product, s and s[1], None if t is None else t[1])
+            one, two, three = (state[which] for which in ("scatter", "finish", "across"))
+            given = gradient_call(state["number"], product, one and one[1], two and two[1], three and three[1])
             state["number"] += 1
-            state["scatter"] = state["across"] = None
-            if t is not None:
-                totals[t[0][0]][t[0][1]] = given["total"]
-            if s is not None:
-                state["across"] = (s[0], given["block"])
+            state["scatter"] = None
+            if three is not None:
+                totals[three[0][0]][three[0][1]] = given["total"]
+            state["across"] = two and (two[0], given["block"])
+            state["finish"] = one and (one[0], (given["kept"], given["third"]))
             if product is not None:
                 shape = (SIDE, SIDE, given["wide"].shape[0] // chips, given["wide"].shape[1])
                 state["scatter"] = ((name, number), (given["wide"].reshape(shape), given["narrow"].reshape(shape)))
@@ -460,8 +585,8 @@
                     lax.dot_general(by, w[i], (((1,), (1,)), ((), ())), preferred_element_type=F32).astype(BF16) for i, by in ((0, by_gate), (1, by_up))
                 ]
                 by_h = by_h + back(by_a[0] + by_a[1])[0]
-        run()
-        run()
+        for _ in range(3):
+            run()
 
         squares = sum(jnp.sum(t.astype(F32) ** 2) for one in totals for t in one)
         squares = plane_sum(state["number"], squares, chips)

time: 880 us -> 784 us (0.89)
  waiting for transfers between devices: 171 us -> 0.77 us
  Pallas kernels: 307 us -> 379 us
    all_gather x6 -> x4, waiting for transfers between devices: 169 us -> 0.01 us  [step(): lax.all_gather(w[number], ('q', 'c'), axis=0, tiled=True)]
    pallas_call x0 -> x1, Pallas kernels: none -> 83.8 us  [gathered_pair(): pl.pallas_call(kernel, out_shape=[jax.ShapeDtypeStruct(shape, BF16)] * 2,...]
    pallas_call x8 -> x9, Pallas kernels: 295 us -> 283 us  [gradient_call(): return dict(zip(names_out, call(*operands), strict=True))]
  transfers between devices with their start and end apart: 12 -> 10, of which waited for: 6 -> 0; matrix products, arithmetic and copies ran while one was open for 21% -> 24% of each run, Pallas kernels for 1% -> 12%
where the time goes in v3:
time: 784 us; the launch traced here: 774 us
  Pallas kernels  379 us (48%)
  matrix products  280 us (36%)
  other arithmetic  48.2 us (6%)
  local copies, waits for them, and re-layouts  31.7 us (4%)
  between operations  19 us (2%)
  starting transfers between devices  15.8 us (2%)
    pallas_call x9, Pallas kernels, gradient_call(): return dict(zip(names_out, call(*operands), strict=True))  283 us
    pallas_call x1, Pallas kernels, gathered_pair(): pl.pallas_call(kernel, out_shape=[jax.ShapeDtypeStruct(shape, BF16)] * 2,...  83.8 us
    dot_general x2, matrix products, step(): up = jnp.dot(a, w[1], preferred_element_type=F32)  80.2 us
    dot_general x2, matrix products, step(): lax.dot_general(by_h, w[2], (((1,), (1,)), ((), ())), preferred_element_t...  69.6 us
    dot_general x2, matrix products, step(): gate = jnp.dot(a, w[0], preferred_element_type=F32)  54.5 us
    dot_general x2, matrix products, step(): lax.dot_general(by, w[i], (((1,), (1,)), ((), ())), preferred_element_typ...  48.3 us
    dot_general x1, matrix products, matmul(): return jnp.dot(a, w, preferred_element_type=F32).astype(BF16)  27.1 us
    unnamed x40, local copies, waits for them, and re-layouts  16.6 us
  transfers between devices with their start and end apart: 10, of which 0 were waited for; matrix products, arithmetic and copies ran while one was open for 24% of the time, Pallas kernels for 12%

profile of v3, /device:TPU:1, one launch (start us, length us, event | category | flops | bytes accessed | tf_op | source)
XLA Modules:
  0.0 774.1 jit_solution(7026349605821739902)
XLA Ops:
  13.4 83.8 %gathered_pair.1 = (bf16[4,4,2,40,3584]{4,3,2,1,0:T(8,128)(2,1)}, bf16[4,4,2,40,3584]{4,3,2,1,0:T(8,128)(2,1)}) custom-call(bf16[2,40,3584]{2,1,0:T(8,128)(2,1)} %one_ref.1, bf16[2,40,3584]{2,1,0:T(8,128)(2,1)} %two_ref.1), custom_call_target="tpu_custom_call" | custom-call | flops 20000000000 | bytes 40000000 | tf_op jit(solution)/shard_map/gathered_pair/pallas_call | solution.py:466
  97.3 7.9 %copy.20 = bf16[1,2048,1280]{1,2,0:T(8,128)(2,1)} copy(bf16[1,2048,1280]{2,1,0:T(8,128)(2,1)} %param.11) | data formatting | bytes 10485760 | tf_op args[0]
  108.8 8.0 %copy.21 = bf16[1,2048,1280]{1,2,0:T(8,128)(2,1)} copy(bf16[1,2048,1280]{2,1,0:T(8,128)(2,1)} %param.12) | data formatting | bytes 10485760 | tf_op args[1]
  116.8 27.1 %fusion.50 = f32[2048,3584]{1,0:T(8,128)} fusion(bf16[1280,3584]{1,0:T(8,128)(2,1)} %bitcast.96, bf16[1,2048,1280]{2,1,0:T(8,128)(2,1)} %param.11, f32[2048]{0:T(1024)S(1)} %add_rsqrt_fusion), kind=kOutput, calls=%fused_computation.55 | convolution fusion | flops 18798346240 | bytes 43786240 | tf_op jit(solution)/shard_map/dot_general | solution.py:548
  150.5 35.3 %multiply_convert_fusion.1 = (bf16[2048,3584]{1,0:T(8,128)(2,1)}, f32[2048,3584]{1,0:T(8,128)}) fusion(f32[2048,3584]{1,0:T(8,128)} %fusion.50, bf16[1280,3584]{1,0:T(8,128)(2,1)} %bitcast.93, bf16[1,2048,1280]{2,1,0:T(8,128)(2,1)} %param.11, f32[2048]{0:T(1024)S(1)} %add_rsqrt_fusion), kind=kOutput, calls=%fused_computation.13 | convolution fusion | flops 18842386432 | bytes 87826432 | tf_op jit(solution)/shard_map/dot_general | solution.py:549
  185.8 27.1 %fusion.12 = (f32[2048]{0:T(1024)S(1)}, bf16[2048,1280]{0,1:T(8,128)(2,1)}) fusion(bf16[2048,3584]{1,0:T(8,128)(2,1)} %get-tuple-element.109.refs_1_, bf16[1,3584,1280]{2,1,0:T(8,128)(2,1)} %all-gather.11.cloned.1.call-done, bf16[1,2048,1280]{1,2,0:T(8,128)(2,1)} %copy.20), kind=kOutput, calls=%fused_computation.29 | convolution fusion | flops 18803587072 | bytes 34349056 | tf_op jit(solution)/shard_map/dot_general | solution.py:20
  213.5 26.1 %convolution_convert_fusion.1 = bf16[2048,3584]{1,0:T(8,128)(2,1)} fusion(bf16[1,3584,1280]{2,1,0:T(8,128)(2,1)} %all-gather.9.cloned.1.call-done, bf16[1,2048,1280]{2,1,0:T(8,128)(2,1)} %param.12), kind=kOutput, calls=%fused_computation.21 | convolution fusion | flops 18797821952 | bytes 29097984 | tf_op jit(solution)/shard_map/dot_general | solution.py:577
  239.5 27.4 %fusion.17 = f32[2048,3584]{1,0:T(8,128)} fusion(bf16[1,1280,3584]{2,1,0:T(8,128)(2,1)} %all-gather.15.cloned.1.call-done, bf16[2048,1280]{0,1:T(8,128)(2,1)} %get-tuple-element.112, f32[2048]{0:T(1024)S(1)} %fusion.64), kind=kOutput, calls=%fused_computation.35 | convolution fusion | flops 18798346240 | bytes 43786240 | tf_op jit(solution)/shard_map/dot_general | solution.py:548
  267.0 44.9 %multiply_convert_fusion = (bf16[2048,3584]{1,0:T(8,128)(2,1)}, bf16[2048,3584]{1,0:T(8,128)(2,1)}, bf16[2048,3584]{1,0:T(8,128)(2,1)}) fusion(f32[2048,3584]{1,0:T(8,128)} %fusion.17, bf16[2048,3584]{1,0:T(8,128)(2,1)} %convolution_convert_fusion.1, bf16[1,1280,3584]{2,1,0:T(8,128)(2,1)} %all-gather.13.cloned.1.call-done, ...), kind=kOutput, calls=%fused_computation.10 | convolution fusion | flops 18915786752 | bytes 102506496 | tf_op jit(solution)/shard_map/dot_general | solution.py:549
  311.9 26.0 %fusion.30 = bf16[2048,1280]{0,1:T(8,128)(2,1)} fusion(bf16[2048,3584]{1,0:T(8,128)(2,1)} %get-tuple-element.94.refs_1_, bf16[1,1280,3584]{2,1,0:T(8,128)(2,1)} %all-gather.13.cloned.1.call-done), kind=kOutput, calls=%fused_computation.46 | convolution fusion | flops 18793103360 | bytes 29097984 | tf_op jit(solution)/shard_map/dot_general | solution.py:585
  337.8 22.4 %fusion.36 = bf16[2048,1280]{0,1:T(8,128)(2,1)S(1)} fusion(bf16[2048,1280]{0,1:T(8,128)(2,1)} %fusion.30, bf16[2048,3584]{1,0:T(8,128)(2,1)} %get-tuple-element.93.refs_1_, bf16[1,1280,3584]{2,1,0:T(8,128)(2,1)S(1)} %copy-done.16), kind=kOutput, calls=%fused_computation.48 | convolution fusion | flops 18795724800 | bytes 34340864 | tf_op jit(solution)/shard_map/dot_general | solution.py:585
  365.5 12.3 %fusion.43 = bf16[2048,1280]{0,1:T(8,128)(2,1)} fusion(bf16[2048,1280]{0,1:T(8,128)(2,1)} %get-tuple-element.112, bf16[2048,1280]{0,1:T(8,128)(2,1)} %copy-done, bf16[1,2048,1280]{1,2,0:T(8,128)(2,1)} %copy.21, f32[2048]{0:T(1024)S(1)} %multiply_multiply_fusion.3, f32[2048]{0:T(1024)S(1)} %fusion.64), kind=kLoop, calls=%fused_computation.51 | loop fusion | flops 18350080 | bytes 20987904 | tf_op jit(solution)/shard_map/add | solution.py:587
  377.9 7.9 %copy.23.refs_0_ = bf16[2048,1280]{1,0:T(8,128)(2,1)} copy(bf16[2048,1280]{0,1:T(8,128)(2,1)} %fusion.43) | data formatting | bytes 10485760 | tf_op jit(solution)/shard_map/add | solution.py:587
  385.7 30.0 %gradient0.1 = (f32[1792,1280]{1,0:T(8,128)}, bf16[1792,1280]{1,0:T(8,128)(2,1)}) custom-call(bf16[2048,1280]{1,0:T(8,128)(2,1)} %bitcast.89, bf16[2048,3584]{1,0:T(8,128)(2,1)} %get-tuple-element.92.refs_1_), custom_call_target="tpu_custom_call" | custom-call | flops 18790481920 | bytes 33685504 | tf_op jit(solution)/shard_map/gradient0/pallas_call | solution.py:372
  415.8 37.2 %gradient1.1 = (f32[1280,1792]{1,0:T(8,128)}, bf16[1280,1792]{1,0:T(8,128)(2,1)}, f32[2,4,112,640]{3,2,1,0:T(8,128)}, bf16[2,112,640]{2,1,0:T(8,128)(2,1)}) custom-call(bf16[1280,2048]{1,0:T(8,128)(2,1)} %get-tuple-element.97.refs_0_, bf16[2048,3584]{1,0:T(8,128)(2,1)} %get-tuple-element.93.refs_1_, f32[4,4,112,1280]{3,2,1,0:T(8,128)} %bitcast.97, ...), custom_call_target="tpu_custom_call" | custom-call | flops 18790481920 | bytes 33685504 | tf_op jit(solution)/shard_map/gradient1/pallas_call | solution.py:372
  453.0 39.8 %gradient2.1 = (f32[1280,1792]{1,0:T(8,128)}, bf16[1280,1792]{1,0:T(8,128)(2,1)}, f32[2,4,80,896]{3,2,1,0:T(8,128)}, bf16[2,80,896]{2,1,0:T(8,128)(2,1)}, bf16[112,1280]{1,0:T(8,128)(2,1)}) custom-call(bf16[1280,2048]{1,0:T(8,128)(2,1)} %get-tuple-element.97.refs_0_, bf16[2048,3584]{1,0:T(8,128)(2,1)} %get-tuple-element.94.refs_1_, ...), custom_call_target="tpu_custom_call" | custom-call | flops 18790481920 | bytes 33685504 | tf_op jit(solution)/shard_map/gradient2/pallas_call | solution.py:372
  492.8 40.4 %gradient3.1 = (f32[1792,1280]{1,0:T(8,128)}, bf16[1792,1280]{1,0:T(8,128)(2,1)}, f32[2,4,80,896]{3,2,1,0:T(8,128)}, bf16[2,80,896]{2,1,0:T(8,128)(2,1)}, bf16[8...) custom-call(bf16[2048,1280]{1,0:T(8,128)(2,1)} %copy.23.refs_0_, bf16[2048,3584]{1,0:T(8,128)(2,1)} %get-tuple-element.109.refs_1_, ...), custom_call_target="tpu_custom_call" | custom-call | flops 18790481920 | bytes 33685504 | tf_op jit(solution)/shard_map/gradient3/pallas_call | solution.py:372
  533.2 43.6 %fusion.5 = (bf16[2048,3584]{1,0:T(8,128)(2,1)}, bf16[2048,3584]{1,0:T(8,128)(2,1)}) fusion(f32[2048,3584]{1,0:T(8,128)} %get-tuple-element.110, f32[2048,3584]{1,0:T(8,128)} %fusion.50, bf16[2048,1280]{0,1:T(8,128)(2,1)} %fusion.43, bf16[1,3584,1280]{2,1,0:T(8,128)(2,1)} %all-gather.11.cloned.1.call-done), kind=kOutput, calls=%fused_computation.9 | convolution fusion | flops 18900582400 | bytes 102498304 | tf_op jit(solution)/shard_map/dot_general | solution.py:577
  576.7 39.9 %gradient4.1 = (f32[1280,1792]{1,0:T(8,128)}, bf16[1280,1792]{1,0:T(8,128)(2,1)}, f32[2,4,112,640]{3,2,1,0:T(8,128)}, bf16[2,112,640]{2,1,0:T(8,128)(2,1)}, bf16...) custom-call(bf16[1280,2048]{1,0:T(8,128)(2,1)} %fusion.44.refs_0_, bf16[2048,3584]{1,0:T(8,128)(2,1)} %get-tuple-element.95.refs_1_, ...), custom_call_target="tpu_custom_call" | custom-call | flops 18790481920 | bytes 33685504 | tf_op jit(solution)/shard_map/gradient4/pallas_call | solution.py:372
  616.7 40.8 %gradient5.1 = (f32[1280,1792]{1,0:T(8,128)}, bf16[1280,1792]{1,0:T(8,128)(2,1)}, f32[2,4,80,896]{3,2,1,0:T(8,128)}, bf16[2,80,896]{2,1,0:T(8,128)(2,1)}, bf16[1...) custom-call(bf16[1280,2048]{1,0:T(8,128)(2,1)} %fusion.44.refs_0_, bf16[2048,3584]{1,0:T(8,128)(2,1)} %get-tuple-element.96.refs_1_, ...), custom_call_target="tpu_custom_call" | custom-call | flops 18790481920 | bytes 33685504 | tf_op jit(solution)/shard_map/gradient5/pallas_call | solution.py:372
  657.5 30.9 %gradient6.1 = (f32[2,4,80,896]{3,2,1,0:T(8,128)}, bf16[2,80,896]{2,1,0:T(8,128)(2,1)}, bf16[80,1792]{1,0:T(8,128)(2,1)}, bf16[112,1280]{1,0:T(8,128)(2,1)}) custom-call(f32[4,4,80,1792]{3,2,1,0:T(8,128)} %bitcast.88, bf16[4,4,80,1792]{3,2,1,0:T(8,128)(2,1)} %bitcast.90, f32[2,4,80,896]{3,2,1,0:T(8,128)} %get-tuple-element.71.refs_2_, ...), custom_call_target="tpu_custom_call" | custom-call | flops 1000000000 | bytes 1000000 | tf_op jit(solution)/shard_map/gradient6/pallas_call | solution.py:372
  688.4 13.3 %gradient7.1 = (bf16[80,1792]{1,0:T(8,128)(2,1)}, bf16[80,1792]{1,0:T(8,128)(2,1)}) custom-call(f32[2,4,80,896]{3,2,1,0:T(8,128)} %get-tuple-element.74.refs_0_, bf16[2,80,896]{2,1,0:T(8,128)(2,1)} %get-tuple-element.75.refs_1_, bf16[80,1792]{1,0:T(8,128)(2,1)} %get-tuple-element.76.refs_2_), custom_call_target="tpu_custom_call" | custom-call | flops 1000000000 | bytes 1000000 | tf_op jit(solution)/shard_map/gradient7/pallas_call | solution.py:372
  708.0 11.0 %gradient8.1 = bf16[80,1792]{1,0:T(8,128)(2,1)} custom-call(bf16[80,1792]{1,0:T(8,128)(2,1)} %get-tuple-element.79.refs_0_), custom_call_target="tpu_custom_call" | custom-call | flops 1000000000 | bytes 1000000 | tf_op jit(solution)/shard_map/gradient8/pallas_call | solution.py:372
  745.2 11.6 %plane_sum.1 = f32[8,128]{1,0:T(8,128)} custom-call(f32[8,128]{1,0:T(8,128)} %broadcast_in_dim.2.value_ref), custom_call_target="tpu_custom_call" | custom-call | tf_op jit(solution)/shard_map/plane_sum/pallas_call | solution.py:510
  (94 shorter events, 60.4 us)
Async XLA Ops:
  7.2 178.6 %all-gather.11.cloned.1.call-start = ((), (), s32[]{:S(2)}) async-start(), calls=%async_computation.1 | async-start | bytes 9461760 | tf_op jit(solution)/shard_map/all_gather | solution.py:541
  9.1 204.3 %all-gather.9.cloned.1.call-start = ((), (), s32[]{:S(2)}) async-start(), calls=%async_computation | async-start | bytes 9461760 | tf_op jit(solution)/shard_map/all_gather | solution.py:541
  9.9 229.6 %all-gather.15.cloned.1.call-start = ((), (), s32[]{:S(2)}) async-start(), calls=%async_computation.3 | async-start | bytes 9461760 | tf_op jit(solution)/shard_map/all_gather | solution.py:541
  11.7 255.3 %all-gather.13.cloned.1.call-start = ((), (), s32[]{:S(2)}) async-start(), calls=%async_computation.2 | async-start | bytes 9461760 | tf_op jit(solution)/shard_map/all_gather | solution.py:541
  311.9 26.0 %copy-start.16 = (bf16[1,1280,3584]{2,1,0:T(8,128)(2,1)S(1)}, bf16[1,1280,3584]{2,1,0:T(8,128)(2,1)}, u32[]{:S(2)}) copy-start(bf16[1,1280,3584]{2,1,0:T(8,128)(2,1)} %all-gather.15.cloned.1.call-done) | copy-start | bytes 27525124
  311.9 48.4 %slice-start = ((s8[5242880]{0:T(1024)(128)(4,1)}), s8[4194304]{0:T(1024)(128)(4,1)S(1)}, s32[]{:S(2)}) async-start(s8[5242880]{0:T(1024)(128)(4,1)} %bitcast.86), calls=%async_computation.4 | async-start | bytes 8388608
  337.8 22.4 %slice-start.1 = ((s8[5242880]{0:T(1024)(128)(4,1)}), s8[1048576]{0:T(1024)(128)(4,1)S(1)}, s32[]{:S(2)}) async-start(s8[5242880]{0:T(1024)(128)(4,1)} %bitcast.86), calls=%async_computation.5 | async-start | bytes 2097152
  360.3 5.3 copy-start
  360.3 5.3 copy-start.15
  657.5 46.0 %copy-start.2 = (bf16[80,1792]{1,0:T(8,128)(2,1)S(1)}, bf16[80,1792]{1,0:T(8,128)(2,1)}, u32[]{:S(2)}) copy-start(bf16[80,1792]{1,0:T(8,128)(2,1)} %get-tuple-element.78) | copy-start | bytes 860164
  688.4 18.2 %copy-start.1 = (bf16[80,1792]{1,0:T(8,128)(2,1)S(1)}, bf16[80,1792]{1,0:T(8,128)(2,1)}, u32[]{:S(2)}) copy-start(bf16[80,1792]{1,0:T(8,128)(2,1)} %get-tuple-element.80) | copy-start | bytes 860164
  701.7 59.1 %copy-start.4 = (bf16[80,1792]{1,0:T(8,128)(2,1)S(1)}, bf16[80,1792]{1,0:T(8,128)(2,1)}, u32[]{:S(2)}) copy-start(bf16[80,1792]{1,0:T(8,128)(2,1)} %get-tuple-element.77) | copy-start | bytes 860164
  707.3 53.8 %copy-start.6 = (bf16[2,40,3584]{2,1,0:T(8,128)(2,1)S(1)}, bf16[2,40,3584]{2,1,0:T(8,128)(2,1)}, u32[]{:S(2)}) copy-start(bf16[2,40,3584]{2,1,0:T(8,128)(2,1)} %one_ref.1) | copy-start | bytes 1720324
  707.3 53.8 %copy-start.7 = (bf16[2,40,3584]{2,1,0:T(8,128)(2,1)S(1)}, bf16[2,40,3584]{2,1,0:T(8,128)(2,1)}, u32[]{:S(2)}) copy-start(bf16[2,40,3584]{2,1,0:T(8,128)(2,1)} %two_ref.1) | copy-start | bytes 1720324
  719.0 41.9 %copy-start.3 = (bf16[80,1792]{1,0:T(8,128)(2,1)S(1)}, bf16[80,1792]{1,0:T(8,128)(2,1)}, u32[]{:S(2)}) copy-start(bf16[80,1792]{1,0:T(8,128)(2,1)} %gradient8.1) | copy-start | bytes 860164
  719.1 42.0 %copy-start.8 = (f32[2,40,3584]{2,1,0:T(8,128)S(1)}, f32[2,40,3584]{2,1,0:T(8,128)}, u32[]{:S(2)}) copy-start(f32[2,40,3584]{2,1,0:T(8,128)} %param.19) | copy-start | bytes 3440644
  722.5 36.9 %collective-permute-start.1 = (bf16[40,1792]{1,0:T(8,128)(2,1)}, bf16[40,1792]{1,0:T(8,128)(2,1)}, u32[]{:S(2)}, u32[]{:S(2)}) collective-permute-start(bf16[40,1792]{1,0:T(8,128)(2,1)} %broadcast_select_fusion.10), channel_id=1, source_target_pairs={{0,1},{1,0},{2,3},{3,2},{4,5},{5,4},{6,7},{7,6},{8,9},{9,8},{10,11... | collective-permute-start | bytes 430088 | tf_op jit(solution)/shard_map/ppermute | solution.py:537
  731.2 33.2 %collective-permute-start.4 = (bf16[112,1280]{1,0:T(8,128)(2,1)}, bf16[112,1280]{1,0:T(8,128)(2,1)}, u32[]{:S(2)}, u32[]{:S(2)}) collective-permute-start(bf16[112,1280]{1,0:T(8,128)(2,1)} %get-tuple-element.81), channel_id=1, source_target_pairs={{0,0},{2,1},{4,2},{6,3},{8,4},{10,5},{12,6},{14,7},{16,8},{18,9},{... | collective-permute-start | bytes 860168 | tf_op jit(solution)/shard_map/ppermute | solution.py:534
  735.3 29.1 %collective-permute-start.5 = (bf16[112,1280]{1,0:T(8,128)(2,1)}, bf16[112,1280]{1,0:T(8,128)(2,1)}, u32[]{:S(2)}, u32[]{:S(2)}) collective-permute-start(bf16[112,1280]{1,0:T(8,128)(2,1)} %get-tuple-element.82), channel_id=1, source_target_pairs={{0,0},{2,1},{4,2},{6,3},{8,4},{10,5},{12,6},{14,7},{16,8},{18,9},{... | collective-permute-start | bytes 860168 | tf_op jit(solution)/shard_map/ppermute | solution.py:534
  756.8 4.3 copy-start.9
  756.8 4.3 copy-start.10
  758.9 2.0 collective-permute-start
  759.3 1.6 collective-permute-start.3
  759.5 1.5 collective-permute-start.2
  (5 other events, 14.7 us)
Sparse Core Ops, SparseCore 0:
  10.8 73.8 all-gather.10
  87.6 55.9 all-gather.8
  146.4 53.9 all-gather.14
  203.1 53.9 all-gather.12
